TPU v7x, 512 devices: a whole 4x8x8 slice. The times are simulated.
512 devices in a mesh: lat: 64 (over x, y, core), lev: 8 (over z).
Axes of the slice: x: 4, y: 8, z: 8, core: 2. Of those that a mesh axis runs over, the one named last changes fastest.
Arguments:
- anomalies: bfloat16 [4, 8, 80, 128, 1536], P(None, 'lev', None, 'lat'), may hold values from -6 to 6
- error_now: float32 [4, 8, 128, 1536], P(None, 'lev', 'lat'), may hold values from -6 to 6
- error_prior: float32 [4, 8, 128, 1536], P(None, 'lev', 'lat'), may hold values from -4.2 to 4.2
- energy_coef: float32 [4, 8], P(None, 'lev'), may hold values from 0.3 to 3
- obs_anomalies: bfloat16 [8192, 80, 256], P('lat', 'lev'), may hold values from -6 to 6
- innovations: float32 [8192, 256], P('lat'), may hold values from -6 to 6
- valid_counts: int32 [8192], P('lat'), may hold values from 0 to 256, as said below
- type_ids: int32 [8192], P('lat'), may hold values from 0 to 7
- error_inverse: float32 [8], replicated, may hold values from 0.25 to 4
Outputs:
- impact: float32 [8192, 16, 256], P('lat', 'lev')
- type_totals: float32 [16, 8], P('lev')
Inputs may be any that keep to these rules, and one draw needn't show every extreme that they name: `valid_counts`: among the 128 slots of each index of lat, the blocks with a positive count come first and the first is always positive; in every draw some index of lat has all 128 slots positive and some block holds 256 rows. Rows below a block's count are observations, the rest padding.
All inputs are finite; a program needn't handle non-finite values.
Results may differ from a plain program's by a relative error of at most 0.0042.
Values may be sent and summed in bfloat16 or wider, within the bound.
A program may use at most 64 MiB of HBM per device.

v0:
```python
import functools
import math

import jax
import jax.numpy as jnp
from jax import lax
from jax.sharding import Mesh
from jax.sharding import PartitionSpec as P

NLAT_GRID = 768
LAT0 = 256
REGIONS = 4
NTYPES = 8
LAT = ("lat_0", "lat_1", "lat_2")
LAT_LEV = ("lat_0", "lat_1", "lat_2", "lev")


def over_axes(array, axes):
    return functools.reduce(lax.psum, axes, array)


def sent_to_all(array, axis):
    copies = jnp.broadcast_to(array, (lax.axis_size(axis), *array.shape))
    return lax.all_to_all(copies, axis, split_axis=0, concat_axis=0, tiled=True)


def taken_together(array, axis):
    return sent_to_all(array, axis).sum(axis=0)


def local(
    anomalies,
    error_now,
    error_prior,
    energy_coef,
    obs_anomalies,
    innovations,
    valid_counts,
    type_ids,
    error_inverse,
):
    lat_rows = error_now.shape[2]
    lat_total = lat_rows * lax.axis_size(LAT)
    lev_total = error_now.shape[1] * lax.axis_size("lev")
    lon_count = error_now.shape[3]
    lat_index = lax.axis_index(LAT) * lat_rows + jnp.arange(lat_rows, dtype=jnp.int32)
    cosine = jnp.cos(
        -0.5 * math.pi + ((lat_index + LAT0).astype(jnp.float32) + 0.5) * math.pi / NLAT_GRID
    )
    gradient = (
        energy_coef[:, :, None, None] * cosine[None, None, :, None] * (error_now + error_prior)
    ).astype(jnp.bfloat16)
    folded = jnp.einsum("vlkji,vlji->vkj", anomalies, gradient, preferred_element_type=jnp.float32)
    region = lat_index * REGIONS // lat_total
    onehot = (region[None, :] == jnp.arange(REGIONS, dtype=jnp.int32)[:, None]).astype(jnp.float32)
    partial_value = jnp.einsum("vkj,rj->vkr", folded, onehot, precision=lax.Precision.HIGHEST)
    summed = over_axes(partial_value, LAT_LEV)
    members = anomalies.shape[2]
    norm_scale = math.sqrt(lev_total * lat_total * lon_count / REGIONS)
    weights = (jnp.transpose(summed, (1, 0, 2)).reshape(members, -1) / norm_scale).astype(
        jnp.bfloat16
    )
    slot_count, local_members, block_rows = obs_anomalies.shape
    lev_groups = lax.axis_size("lev")
    grouped = obs_anomalies.reshape(lev_groups, slot_count // lev_groups, local_members, block_rows)
    answered = jnp.einsum(
        "gbks,kt->gbts",
        lax.all_to_all(grouped, "lev", split_axis=0, concat_axis=2, tiled=True),
        weights,
        preferred_element_type=jnp.float32,
    )
    response = lax.all_to_all(answered[0], "lev", split_axis=1, concat_axis=0, tiled=True)
    type_table = type_ids[:, None] == jnp.arange(NTYPES, dtype=jnp.int32)[None, :]
    inverse_var = jnp.sum(
        jnp.where(type_table, error_inverse[None, :], jnp.zeros((), jnp.float32)), axis=1
    )
    positions = jnp.arange(block_rows, dtype=jnp.int32)
    row_mask = (positions[None, :] < valid_counts[:, None]).astype(jnp.float32)
    scaling = innovations * inverse_var[:, None] * row_mask / math.sqrt(members - 1)
    impact = response * scaling[:, None, :]
    per_block = jnp.sum(impact, axis=2)
    local_totals = jnp.dot(
        per_block.T, type_table.astype(jnp.float32), precision=lax.Precision.HIGHEST
    )
    block_total = slot_count * lax.axis_size(LAT)
    type_totals = taken_together(local_totals, LAT) / math.sqrt(block_total * block_rows / NTYPES)
    return (impact, type_totals)


def solution(mesh):
    split = Mesh(
        mesh.devices.reshape(4, 8, 2, mesh.shape["lev"]), ("lat_0", "lat_1", "lat_2", "lev")
    )
    in_specs = (
        P(None, "lev", None, LAT, None),
        P(None, "lev", LAT, None),
        P(None, "lev", LAT, None),
        P(None, "lev"),
        P(LAT, "lev", None),
        P(LAT, None),
        P(LAT),
        P(LAT),
        P(),
    )
    out_specs = (P(LAT, "lev", None), P("lev", None))
    return jax.shard_map(local, mesh=split, in_specs=in_specs, out_specs=out_specs, check_vma=False)
```

profile of v0, /device:TPU:1, one launch (start us, length us, event | category | flops | bytes accessed | tf_op | source)
XLA Modules:
  0.0 97.7 jit_solution(9354519647972470632)
XLA Ops:
  0.6 0.0 copy-start
  0.6 0.0 copy-start.5
  0.7 0.0 copy-start.2
  0.7 0.0 copy-start.3
  0.7 2.1 %copy.41 = bf16[8,16,10,256]{3,1,2,0:T(8,128)(2,1)} copy(bf16[8,16,10,256]{3,1,0,2:T(8,128)(2,1)} %bitcast.49) | data formatting | bytes 1310720 | tf_op jit(solution)/shard_map/reshape | solution.py:65
  2.8 10.9 %all-to-all-start = ((bf16[8,16,10,256]{3,1,2,0:T(8,128)(2,1)}), bf16[8,16,10,256]{3,1,2,0:T(8,128)(2,1)S(1)}, u32[]{:S(2)}, u32[]{:S(2)}) async-start(bf16[8,16,10,256]{3,1,2,0:T(8,128)(2,1)} %copy.41), calls=%async_computation | async-start | bytes 1310720 | tf_op jit(solution)/shard_map/all_to_all | solution.py:68
  13.7 0.0 copy-done.5
  13.7 0.1 broadcast_multiply_fusion
  13.8 0.0 copy-done.2
  13.8 0.0 copy-done.3
  13.8 0.1 fusion.5
  13.9 0.0 copy-done
  13.9 0.0 copy-start.6
  13.9 0.0 copy-start.7
  13.9 0.0 copy-start.1
  13.9 0.0 copy-start.4
  13.9 0.6 fusion
  14.6 0.3 fusion.8
  14.8 8.9 %psum.28 = f32[4,80,4]{1,2,0:T(4,128)S(1)} all-reduce(f32[4,80,4]{1,2,0:T(4,128)S(1)} %fusion.8), channel_id=1, replica_groups=mesh['lat_0'=4,'lat_1'=8,'lat_2'=2,'lev'=8] {'lat_0'}, use_global_device_ids=true, to_apply=%region_0.1 | all-reduce | flops 1280 | bytes 10240 | tf_op jit(solution)/shard_map/psum | solution.py:19
  23.7 14.7 %psum.29 = f32[4,80,4]{1,2,0:T(4,128)S(1)} all-reduce(f32[4,80,4]{1,2,0:T(4,128)S(1)} %psum.28), channel_id=1, replica_groups=mesh['lat_0'=4,'lat_1'=8,'lat_2'=2,'lev'=8] {'lat_1'}, use_global_device_ids=true, to_apply=%region_1.2 | all-reduce | flops 1280 | bytes 10240 | tf_op jit(solution)/shard_map/psum | solution.py:19
  38.4 8.0 %psum.30 = f32[4,80,4]{1,2,0:T(4,128)S(1)} all-reduce(f32[4,80,4]{1,2,0:T(4,128)S(1)} %psum.29), channel_id=1, replica_groups=mesh['lat_0'=4,'lat_1'=8,'lat_2'=2,'lev'=8] {'lat_2'}, use_global_device_ids=true, to_apply=%region_2.3 | all-reduce | flops 1280 | bytes 10240 | tf_op jit(solution)/shard_map/psum | solution.py:19
  46.4 14.2 %psum.31 = f32[4,80,4]{1,2,0:T(4,128)S(1)} all-reduce(f32[4,80,4]{1,2,0:T(4,128)S(1)} %psum.30), channel_id=1, replica_groups=mesh['lat_0'=4,'lat_1'=8,'lat_2'=2,'lev'=8] {'lev'}, use_global_device_ids=true, to_apply=%region_3.4 | all-reduce | flops 1280 | bytes 10240 | tf_op jit(solution)/shard_map/psum | solution.py:19
  60.7 0.0 all-to-all-done
  60.7 0.3 convolution_bitcast_fusion
  61.0 0.9 copy.43
  61.8 3.9 %all-to-all-start.1 = ((f32[16,16,256]{2,0,1:T(8,128)}), f32[16,16,256]{2,0,1:T(8,128)S(1)}, u32[]{:S(2)}, u32[]{:S(2)}) async-start(f32[16,16,256]{2,0,1:T(8,128)} %copy.43), calls=%async_computation.1 | async-start | bytes 524288 | tf_op jit(solution)/shard_map/all_to_all | solution.py:72
  65.7 0.0 copy-done.6
  65.7 0.0 copy-done.7
  65.7 0.1 select_reduce_fusion
  65.8 0.0 copy-done.1
  65.8 0.0 copy-done.4
  65.8 0.1 select_multiply_fusion
  65.9 0.1 copy.46
  66.0 9.0 %all-to-all-done.1 = f32[16,16,256]{2,0,1:T(8,128)S(1)} async-done(((f32[16,16,256]{2,0,1:T(8,128)}), f32[16,16,256]{2,0,1:T(8,128)S(1)}, u32[]{:S(2)}, u32[]{:S(2)}) %all-to-all-start.1) | async-done | bytes 262176 | tf_op jit(solution)/shard_map/all_to_all | solution.py:72
  75.1 0.2 copy.52
  75.3 0.3 fusion.3
  75.6 0.1 copy.47
  75.7 0.1 reduce_sum.31
  75.8 0.1 fusion.6
  75.9 0.7 broadcast_in_dim.16
  76.6 10.7 %all-to-all-start.2 = ((f32[64,2,8]{2,1,0:T(2,128)}), f32[64,2,8]{2,1,0:T(2,128)S(1)}, u32[]{:S(2)}, u32[]{:S(2)}) async-start(f32[64,2,8]{2,1,0:T(2,128)} %broadcast_in_dim.16), calls=%async_computation.2 | async-start | bytes 131072 | tf_op jit(solution)/shard_map/all_to_all | solution.py:24
  87.2 0.9 bitcast_multiply_fusion
  88.1 8.9 %all-to-all-done.2 = f32[64,2,8]{2,1,0:T(2,128)S(1)} async-done(((f32[64,2,8]{2,1,0:T(2,128)}), f32[64,2,8]{2,1,0:T(2,128)S(1)}, u32[]{:S(2)}, u32[]{:S(2)}) %all-to-all-start.2) | async-done | bytes 4128 | tf_op jit(solution)/shard_map/all_to_all | solution.py:24
  97.0 0.1 reduce_sum.32
  97.1 0.6 broadcast_multiply_fusion.1
  (3 shorter events, 0.1 us)
Async XLA Ops:
  0.6 13.3 %copy-start = (bf16[4,1,80,2,1536]{4,3,2,1,0:T(2,128)(2,1)S(1)}, bf16[4,1,80,2,1536]{4,3,2,1,0:T(2,128)(2,1)}, u32[]{:S(2)}) copy-start(bf16[4,1,80,2,1536]{4,3,2,1,0:T(2,128)(2,1)} %param.9) | copy-start | bytes 5898244
  0.6 13.1 %copy-start.5 = (f32[4,1]{0,1:T(1,128)S(1)}, f32[4,1]{0,1:T(1,128)}, u32[]{:S(2)}) copy-start(f32[4,1]{0,1:T(1,128)} %param.12) | copy-start | bytes 52
  0.7 13.1 %copy-start.2 = (f32[4,1,2,1536]{3,2,1,0:T(2,128)S(1)}, f32[4,1,2,1536]{3,2,1,0:T(2,128)}, u32[]{:S(2)}) copy-start(f32[4,1,2,1536]{3,2,1,0:T(2,128)} %param.10) | copy-start | bytes 147460
  0.7 13.1 %copy-start.3 = (f32[4,1,2,1536]{3,2,1,0:T(2,128)S(1)}, f32[4,1,2,1536]{3,2,1,0:T(2,128)}, u32[]{:S(2)}) copy-start(f32[4,1,2,1536]{3,2,1,0:T(2,128)} %param.11) | copy-start | bytes 147460
  2.8 57.9 %all-to-all-start = ((bf16[8,16,10,256]{3,1,2,0:T(8,128)(2,1)}), bf16[8,16,10,256]{3,1,2,0:T(8,128)(2,1)S(1)}, u32[]{:S(2)}, u32[]{:S(2)}) async-start(bf16[8,16,10,256]{3,1,2,0:T(8,128)(2,1)} %copy.41), calls=%async_computation | async-start | bytes 1310720 | tf_op jit(solution)/shard_map/all_to_all | solution.py:68
  13.9 51.8 %copy-start.6 = (f32[8]{0:T(128)S(1)}, f32[8]{0:T(128)}, u32[]{:S(2)}) copy-start(f32[8]{0:T(128)} %param.17) | copy-start | bytes 100
  13.9 51.8 %copy-start.7 = (s32[128]{0:T(128)S(1)}, s32[128]{0:T(128)}, u32[]{:S(2)}) copy-start(s32[128]{0:T(128)} %param.16) | copy-start | bytes 1540
  13.9 51.9 %copy-start.1 = (f32[128,256]{1,0:T(8,128)S(1)}, f32[128,256]{1,0:T(8,128)}, u32[]{:S(2)}) copy-start(f32[128,256]{1,0:T(8,128)} %param.14) | copy-start | bytes 393220
  13.9 51.9 %copy-start.4 = (s32[128]{0:T(128)S(1)}, s32[128]{0:T(128)}, u32[]{:S(2)}) copy-start(s32[128]{0:T(128)} %param.15) | copy-start | bytes 1540
  61.8 13.2 %all-to-all-start.1 = ((f32[16,16,256]{2,0,1:T(8,128)}), f32[16,16,256]{2,0,1:T(8,128)S(1)}, u32[]{:S(2)}, u32[]{:S(2)}) async-start(f32[16,16,256]{2,0,1:T(8,128)} %copy.43), calls=%async_computation.1 | async-start | bytes 524288 | tf_op jit(solution)/shard_map/all_to_all | solution.py:72
  76.6 20.5 %all-to-all-start.2 = ((f32[64,2,8]{2,1,0:T(2,128)}), f32[64,2,8]{2,1,0:T(2,128)S(1)}, u32[]{:S(2)}, u32[]{:S(2)}) async-start(f32[64,2,8]{2,1,0:T(2,128)} %broadcast_in_dim.16), calls=%async_computation.2 | async-start | bytes 131072 | tf_op jit(solution)/shard_map/all_to_all | solution.py:24
where the time goes:
time: 98.1 us; the launch traced here: 97.7 us
  blocking collectives  45.8 us (47%)
  starting transfers between devices  25.4 us (26%)
  waiting for transfers between devices  18 us (18%)
  local copies, waits for them, and re-layouts  4.17 us (4%)
  other arithmetic  2.21 us (2%)
  matrix products  1.28 us (1%)
    psum x4, blocking collectives, over_axes(): return functools.reduce(lax.psum, axes, array)  45.8 us
    all_to_all x1, starting transfers between devices, local(): lax.all_to_all(grouped, 'lev', split_axis=0, concat_axis=2, tiled=True)  10.9 us
    all_to_all x1, starting transfers between devices, sent_to_all(): return lax.all_to_all(copies, axis, split_axis=0, concat_axis=0, tiled=True)  10.7 us
    all_to_all x1, waiting for transfers between devices, local(): lax.all_to_all(answered[0], 'lev', split_axis=1, concat_axis=0, tiled=True)  9.03 us
    all_to_all x1, waiting for transfers between devices, sent_to_all(): return lax.all_to_all(copies, axis, split_axis=0, concat_axis=0, tiled=True)  8.92 us
    all_to_all x1, starting transfers between devices, local(): lax.all_to_all(answered[0], 'lev', split_axis=1, concat_axis=0, tiled=True)  3.89 us
    reshape x1, local copies, waits for them, and re-layouts, local(): obs_anomalies.reshape(lev_groups, slot_count // lev_groups, local_members...  2.12 us
  transfers between devices with their start and end apart: 3, of which 2 were waited for; matrix products, arithmetic and copies ran while one was open for 2% of the time, Pallas kernels for 0%

commit v1 on v0

v1 whole, which is shorter than its diff:
```python
import functools
import math

import jax
import jax.numpy as jnp
from jax import lax
from jax.experimental import pallas as pl
from jax.experimental.pallas import tpu as pltpu
from jax.sharding import Mesh
from jax.sharding import PartitionSpec as P

NLAT_GRID = 768
LAT0 = 256
REGIONS = 4
NTYPES = 8
LAT = ("lat_0", "lat_1", "lat_2")
MESH = pl.DeviceIdType.MESH
F32 = jnp.float32
BF16 = jnp.bfloat16


def ring_order(n):
    return sorted(range(1, n), key=lambda d: (-min(d, n - d), d))


def exchange_kernel(
    dims,
    norm_scale,
    total_scale,
    part_ref,
    obs_v,
    scal_ref,
    type_ref,
    out_ref,
    tot_ref,
    mz,
    my,
    mx,
    mz_src,
    my_src,
    mx_src,
    obs_in,
    wd,
    resp_src,
    resp_in,
    pt_src,
    pt_in,
    mz_send,
    mz_recv,
    my_send,
    my_recv,
    mx_send,
    mx_recv,
    ob_send,
    ob_recv,
    rs_send,
    rs_recv,
    pt_send,
    pt_recv,
):
    nx, ny, nc, nz = dims
    members, slots, rows = obs_v.shape
    own = slots // nz
    targets = 16
    pair = targets // nz
    xi = lax.axis_index("lat_0")
    yi = lax.axis_index("lat_1")
    ci = lax.axis_index("lat_2")
    zi = lax.axis_index("lev")

    def z_peer(d):
        return {"lev": lax.rem(zi + d, nz)}

    def x_peer(d):
        return {"lat_0": lax.rem(xi + d, nx)}

    def y_peer(d, e):
        return {"lat_1": lax.rem(yi + d, ny), "lat_2": lax.rem(ci + e, nc)}

    y_steps = [(d, e) for d in ring_order(ny) + [0] for e in range(nc) if d or e]
    barrier = pltpu.get_barrier_semaphore()
    peers = [z_peer(d) for d in ring_order(nz)]
    peers += [y_peer(d, e) for d, e in y_steps]
    peers += [x_peer(d) for d in ring_order(nx)]
    for peer in peers:
        pl.semaphore_signal(barrier, inc=1, device_id=peer, device_id_type=MESH)

    onehot = (
        lax.broadcasted_iota(jnp.int32, (NTYPES, slots), 0) == type_ref[...]
    ).astype(F32)
    lane4 = lax.broadcasted_iota(jnp.int32, (4, 128), 1)
    payload = part_ref[...]
    base = payload
    g_add = jnp.zeros((4, 128), F32)
    scal = scal_ref[...]
    for m in range(members):
        prod = obs_v[m].astype(F32) * scal
        by_type = jnp.dot(
            onehot, prod, precision=lax.Precision.HIGHEST, preferred_element_type=F32
        )
        g = jnp.sum(by_type, axis=1, keepdims=True)
        g_add = jnp.where(lane4 == 80 + m, g[0:4], g_add)
        g_add = jnp.where(lane4 == 90 + m, g[4:8], g_add)
    mz_src[0] = base
    mz[pl.ds(zi, 1)] = base[None]

    mine = pl.ds(pl.multiple_of(zi * own, own), own)
    obs_in[pl.ds(zi, 1)] = obs_v[:, mine, :][None]

    pl.semaphore_wait(barrier, len(peers))

    z_copies = []
    for d in ring_order(nz):
        copy = pltpu.make_async_remote_copy(
            src_ref=mz_src.at[0],
            dst_ref=mz.at[zi],
            send_sem=mz_send.at[d],
            recv_sem=mz_recv.at[d],
            device_id=z_peer(d),
            device_id_type=MESH,
        )
        copy.start()
        z_copies.append(copy)
    ob_copies = []
    for d in ring_order(nz):
        other = lax.rem(zi + d, nz)
        there = pl.ds(pl.multiple_of(other * own, own), own)
        copy = pltpu.make_async_remote_copy(
            src_ref=obs_v.at[:, there, :],
            dst_ref=obs_in.at[zi],
            send_sem=ob_send.at[d],
            recv_sem=ob_recv.at[d],
            device_id=z_peer(d),
            device_id_type=MESH,
        )
        copy.start()
        ob_copies.append(copy)

    sel_cols = nz * members * own
    sel = (
        lax.broadcasted_iota(jnp.int32, (128, sel_cols), 0)
        == lax.broadcasted_iota(jnp.int32, (128, sel_cols), 1) // own
    ).astype(BF16)
    row_t = lax.broadcasted_iota(jnp.int32, (targets * own, targets), 0) // own
    col_t = lax.broadcasted_iota(jnp.int32, (targets * own, targets), 1)
    spread = (col_t == lax.rem(row_t, REGIONS) * 4 + row_t // REGIONS).astype(BF16)
    sel_z = (
        lax.broadcasted_iota(jnp.int32, (128, 128), 0)
        == lax.broadcasted_iota(jnp.int32, (128, 128), 1) + zi * members
    ) & (lax.broadcasted_iota(jnp.int32, (128, 128), 1) < members)
    sel_z = sel_z.astype(BF16)
    perm_r = lax.broadcasted_iota(jnp.int32, (targets, targets), 0)
    perm_c = lax.broadcasted_iota(jnp.int32, (targets, targets), 1)
    perm = (perm_c == lax.rem(perm_r, REGIONS) * 4 + perm_r // REGIONS).astype(BF16)

    for copy in z_copies:
        copy.wait()
    tot_z = mz[0]
    for z in range(1, nz):
        tot_z = tot_z + mz[z]
    tot_z = tot_z + g_add
    my_src[0] = tot_z
    here_y = yi * nc + ci
    my[pl.ds(here_y, 1)] = tot_z[None]
    y_copies = []
    for d, e in y_steps:
        copy = pltpu.make_async_remote_copy(
            src_ref=my_src.at[0],
            dst_ref=my.at[here_y],
            send_sem=my_send.at[d * nc + e],
            recv_sem=my_recv.at[d * nc + e],
            device_id=y_peer(d, e),
            device_id_type=MESH,
        )
        copy.start()
        y_copies.append(copy)
    for copy in y_copies:
        copy.wait()
    tot_y = my[0]
    for y in range(1, ny * nc):
        tot_y = tot_y + my[y]
    mx_src[0] = tot_y
    mx[pl.ds(xi, 1)] = tot_y[None]
    x_copies = []
    for d in ring_order(nx):
        copy = pltpu.make_async_remote_copy(
            src_ref=mx_src.at[0],
            dst_ref=mx.at[xi],
            send_sem=mx_send.at[d],
            recv_sem=mx_recv.at[d],
            device_id=x_peer(d),
            device_id_type=MESH,
        )
        copy.start()
        x_copies.append(copy)
    for copy in x_copies:
        copy.wait()

    sums = jnp.concatenate([mx[x] for x in range(nx)], axis=0)
    lane16 = lax.broadcasted_iota(jnp.int32, (targets, 128), 1)
    w = jnp.where(lane16 < 80, sums / norm_scale, 0.0).astype(BF16)
    g_all = mx[0]
    for x in range(1, nx):
        g_all = g_all + mx[x]

    wide = jnp.dot(w, sel, preferred_element_type=F32).astype(BF16)
    tall = jnp.dot(spread, wide, preferred_element_type=F32)
    shape = (targets * own, sel_cols)
    keep = lax.rem(lax.broadcasted_iota(jnp.int32, shape, 0), own) == lax.rem(
        lax.broadcasted_iota(jnp.int32, shape, 1), own
    )
    wd[...] = jnp.where(keep, tall, 0.0).astype(BF16)

    for copy in ob_copies:
        copy.wait()
    gathered = obs_in[...].reshape(sel_cols, rows)
    answered = jnp.dot(wd[...], gathered, preferred_element_type=F32)
    resp_src[...] = answered.astype(BF16).reshape(nz, pair, own, rows)
    rs_copies = []
    for d in ring_order(nz):
        other = lax.rem(zi + d, nz)
        copy = pltpu.make_async_remote_copy(
            src_ref=resp_src.at[other],
            dst_ref=resp_in.at[zi],
            send_sem=rs_send.at[d],
            recv_sem=rs_recv.at[d],
            device_id=z_peer(d),
            device_id_type=MESH,
        )
        copy.start()
        rs_copies.append(copy)
    resp_in[pl.ds(zi, 1)] = resp_src[pl.ds(zi, 1)]

    w_own = jnp.dot(w, sel_z, preferred_element_type=F32).astype(BF16)
    w_own = jnp.dot(perm, w_own, preferred_element_type=F32)
    g_low = pltpu.roll(g_all, 128 - 80, 1)
    g_high = pltpu.roll(g_all, 128 - 90, 1)
    g_rows = jnp.concatenate([g_low, g_high], axis=0)
    lane8 = lax.broadcasted_iota(jnp.int32, (NTYPES, 128), 1)
    g_rows = jnp.where(lane8 < members, g_rows, 0.0)
    lanes = lax.broadcasted_iota(jnp.int32, (targets, 128), 1)
    share = jnp.zeros((targets, 128), F32)
    for c in range(NTYPES):
        col = jnp.sum(w_own * g_rows[c : c + 1], axis=1, keepdims=True)
        share = jnp.where(lanes == c, col, share)
    for z in range(nz):
        pt_src[z, 0:pair, :] = share[pair * z : pair * z + pair]
    pt_copies = []
    for d in ring_order(nz):
        other = lax.rem(zi + d, nz)
        copy = pltpu.make_async_remote_copy(
            src_ref=pt_src.at[other, pl.ds(0, pair)],
            dst_ref=pt_in.at[zi, pl.ds(0, pair)],
            send_sem=pt_send.at[d],
            recv_sem=pt_recv.at[d],
            device_id=z_peer(d),
            device_id_type=MESH,
        )
        copy.start()
        pt_copies.append(copy)
    pt_in[pl.ds(zi, 1), 0:pair, :] = pt_src[pl.ds(zi, 1), 0:pair, :]

    for copy in rs_copies:
        copy.wait()
    for z in range(nz):
        for t in range(pair):
            value = resp_in[z, t].astype(F32) * scal_ref[z * own : (z + 1) * own, :]
            for half in range(2):
                out_ref[pl.ds(z * own * 4 + half * 2 + t, own, stride=4), :] = value[
                    :, half * 128 : (half + 1) * 128
                ]
    for copy in pt_copies:
        copy.wait()
    whole = pt_in[0, 0:pair, :]
    for z in range(1, nz):
        whole = whole + pt_in[z, 0:pair, :]
    tot_ref[...] = whole[:, 0:NTYPES] / total_scale


def local(
    anomalies,
    error_now,
    error_prior,
    energy_coef,
    obs_anomalies,
    innovations,
    valid_counts,
    type_ids,
    error_inverse,
):
    dims = tuple(lax.axis_size(a) for a in (*LAT, "lev"))
    lat_rows = error_now.shape[2]
    lat_total = lat_rows * lax.axis_size(LAT)
    lev_total = error_now.shape[1] * lax.axis_size("lev")
    lon_count = error_now.shape[3]
    lat_index = lax.axis_index(LAT) * lat_rows + jnp.arange(lat_rows, dtype=jnp.int32)
    cosine = jnp.cos(
        -0.5 * math.pi + ((lat_index + LAT0).astype(F32) + 0.5) * math.pi / NLAT_GRID
    )
    gradient = (
        energy_coef[:, :, None, None] * cosine[None, None, :, None] * (error_now + error_prior)
    ).astype(BF16)
    folded = jnp.einsum("vlkji,vlji->vk", anomalies, gradient, preferred_element_type=F32)
    members = anomalies.shape[2]
    variables = anomalies.shape[0]
    part = jnp.pad(folded, ((0, 0), (0, 128 - members)))
    norm_scale = math.sqrt(lev_total * lat_total * lon_count / REGIONS)
    slots, local_members, rows = obs_anomalies.shape
    type_table = type_ids[:, None] == jnp.arange(NTYPES, dtype=jnp.int32)[None, :]
    inverse_var = jnp.sum(
        jnp.where(type_table, error_inverse[None, :], jnp.zeros((), F32)), axis=1
    )
    positions = jnp.arange(rows, dtype=jnp.int32)
    row_mask = (positions[None, :] < valid_counts[:, None]).astype(F32)
    scaling = innovations * inverse_var[:, None] * row_mask / math.sqrt(members - 1)
    total_scale = math.sqrt(slots * lax.axis_size(LAT) * rows / NTYPES)
    nx, ny, nc, nz = dims
    own = slots // nz
    targets = variables * REGIONS
    pair = targets // nz
    vmem = pl.BlockSpec(memory_space=pltpu.VMEM)
    dma = pltpu.SemaphoreType.DMA
    out, totals = pl.pallas_call(
        functools.partial(exchange_kernel, dims, norm_scale, total_scale),
        out_shape=(
            jax.ShapeDtypeStruct((slots * pair * rows // 128, 128), F32),
            jax.ShapeDtypeStruct((pair, NTYPES), F32),
        ),
        in_specs=[vmem, vmem, vmem, vmem],
        out_specs=(vmem, vmem),
        scratch_shapes=[
            pltpu.VMEM((nz, 4, 128), F32),
            pltpu.VMEM((ny * nc, 4, 128), F32),
            pltpu.VMEM((nx, 4, 128), F32),
            pltpu.VMEM((1, 4, 128), F32),
            pltpu.VMEM((1, 4, 128), F32),
            pltpu.VMEM((1, 4, 128), F32),
            pltpu.VMEM((nz, local_members, own, rows), BF16),
            pltpu.VMEM((targets * own, nz * local_members * own), BF16),
            pltpu.VMEM((nz, pair, own, rows), BF16),
            pltpu.VMEM((nz, pair, own, rows), BF16),
            pltpu.VMEM((nz, 8, 128), F32),
            pltpu.VMEM((nz, 8, 128), F32),
            dma((nz,)),
            dma((nz,)),
            dma((ny * nc,)),
            dma((ny * nc,)),
            dma((nx,)),
            dma((nx,)),
            dma((nz,)),
            dma((nz,)),
            dma((nz,)),
            dma((nz,)),
            dma((nz,)),
            dma((nz,)),
        ],
        compiler_params=pltpu.CompilerParams(
            collective_id=0, has_side_effects=True, vmem_limit_bytes=32 * 1024 * 1024
        ),
    )(part, jnp.transpose(obs_anomalies, (1, 0, 2)), scaling, type_ids.reshape(1, slots))
    impact = out.reshape(slots, rows // 128, pair, 128)
    impact = jnp.transpose(impact, (0, 2, 1, 3)).reshape(slots, pair, rows)
    return (impact, totals)


def solution(mesh):
    split = Mesh(
        mesh.devices.reshape(4, 8, 2, mesh.shape["lev"]), ("lat_0", "lat_1", "lat_2", "lev")
    )
    in_specs = (
        P(None, "lev", None, LAT, None),
        P(None, "lev", LAT, None),
        P(None, "lev", LAT, None),
        P(None, "lev"),
        P(LAT, "lev", None),
        P(LAT, None),
        P(LAT),
        P(LAT),
        P(),
    )
    out_specs = (P(LAT, "lev", None), P("lev", None))
    return jax.shard_map(local, mesh=split, in_specs=in_specs, out_specs=out_specs, check_vma=False)
```

time: 98.1 us -> 44.6 us (0.45)
  blocking collectives: 45.8 us -> 0 us
  Pallas kernels: 0 us -> 37.5 us
  starting transfers between devices: 25.4 us -> 0 us
  waiting for transfers between devices: 18 us -> 0 us
  local copies, waits for them, and re-layouts: 4.17 us -> 2.82 us
    psum x4 -> x0, blocking collectives: 45.8 us -> none  [over_axes(): return functools.reduce(lax.psum, axes, array)]
    pallas_call x0 -> x1, Pallas kernels: none -> 37.5 us  [local(): pl.pallas_call(functools.partial(exchange_kernel, dims, norm_scale, total...]
    all_to_all x3 -> x0, starting transfers between devices: 25.4 us -> none  [the longest x1 10.9 us: local(): lax.all_to_all(grouped, 'lev', split_axis=0, concat_axis=2, tiled=True)]
    all_to_all x3 -> x0, waiting for transfers between devices: 18 us -> none  [the longest x1 9.03 us: local(): lax.all_to_all(answered[0], 'lev', split_axis=1, concat_axis=0, tiled=True)]
    unnamed x16 -> x12, local copies, waits for them, and re-layouts: 0.05 us -> 2.81 us
    reshape x1 -> x0, local copies, waits for them, and re-layouts: 2.12 us -> none  [local(): obs_anomalies.reshape(lev_groups, slot_count // lev_groups, local_members...]
  transfers between devices with their start and end apart: 3 -> 0, of which waited for: 2 -> 0; matrix products, arithmetic and copies ran while one was open for 2% -> 0% of each run, Pallas kernels for 0% -> 0%
where the time goes in v1:
time: 44.6 us; the launch traced here: 44.2 us
  Pallas kernels  37.5 us (84%)
  local copies, waits for them, and re-layouts  2.82 us (6%)
  other arithmetic  2.53 us (6%)
  between operations  0.73 us (2%)
  matrix products  0.61 us (1%)
    pallas_call x1, Pallas kernels, local(): pl.pallas_call(functools.partial(exchange_kernel, dims, norm_scale, total...  37.5 us
    unnamed x12, local copies, waits for them, and re-layouts  2.81 us
    another operation x1, other arithmetic  0.91 us

profile of v1, /device:TPU:1, one launch (start us, length us, event | category | flops | bytes accessed | tf_op | source)
XLA Modules:
  0.0 44.2 jit_solution(11837825732267744395)
XLA Ops:
  0.6 0.0 copy-start
  0.6 0.0 copy-start.2
  0.7 0.0 copy-start.4
  0.7 0.0 copy-start.3
  0.7 0.0 copy-start.1
  0.7 1.5 %copy-done = bf16[4,1,80,2,1536]{4,3,2,1,0:T(2,128)(2,1)S(1)} copy-done((bf16[4,1,80,2,1536]{4,3,2,1,0:T(2,128)(2,1)S(1)}, bf16[4,1,80,2,1536]{4,3,2,1,0:T(2,128)(2,1)}, u32[]{:S(2)}) %copy-start) | copy-done | bytes 1966104
  2.3 0.8 %select_reduce_fusion = f32[128]{0:T(128)S(1)} fusion(f32[8]{0:T(128)} %param.17, s32[128]{0:T(128)} %param.16), kind=kLoop, calls=%fused_computation.7 | loop fusion | flops 2944 | bytes 1056 | tf_op jit(solution)/shard_map/reduce_sum | solution.py:310
  3.0 0.7 %broadcast_multiply_fusion = f32[4,2]{1,0:T(4,128)S(1)} fusion(f32[2]{0:T(128)S(1)} %add_cosine_fusion, f32[4]{0:T(128)} %bitcast.20), kind=kLoop, calls=%fused_computation.9 | loop fusion | flops 8 | bytes 56 | tf_op jit(solution)/shard_map/mul | solution.py:301
  3.7 0.9 %fusion.3 = bf16[4,2,1536,1]{2,1,0,3:T(2,128)(2,1)S(1)} fusion(f32[4,1,2,1536]{3,2,1,0:T(2,128)} %param.10, f32[4,1,2,1536]{3,2,1,0:T(2,128)} %param.11, f32[4,2]{1,0:T(4,128)S(1)} %broadcast_multiply_fusion), kind=kLoop, calls=%fused_computation.6 | loop fusion | flops 36864 | bytes 122912 | tf_op jit(solution)/shard_map/reshape.7
  4.6 0.6 %fusion = f32[4,1,80,1]{2,1,3,0:T(1,128)S(1)} fusion(bf16[4,80,2,1536]{3,2,1,0:T(2,128)(2,1)S(1)} %bitcast.15, bf16[4,2,1536,1]{2,1,0,3:T(2,128)(2,1)S(1)} %fusion.3), kind=kOutput, calls=%fused_computation | convolution fusion | flops 1966080 | bytes 1991936 | tf_op jit(solution)/shard_map/vlkji,vlji->vk/dot_general | solution.py:303
  5.3 0.0 copy-done.4
  5.3 0.0 copy-done.3
  5.3 0.1 select_multiply_fusion.scal_ref
  5.4 0.0 copy-done.2
  5.4 0.0 copy-done.1
  5.4 37.5 %shard_map.104 = (f32[512,128]{1,0:T(8,128)S(1)}, f32[2,8]{1,0:T(2,128)S(1)}) custom-call(f32[4,128]{1,0:T(4,128)S(1)} %pad.4.part_ref, bf16[10,128,256]{2,1,0:T(8,128)(2,1)S(1)} %bitcast.16, f32[128,256]{1,0:T(8,128)S(1)} %select_multiply_fusion.scal_ref, s32[1,128]{1,0:T(1,128)S(1)} %bitcast.18), custom_call_target="tpu_custom_call" | custom-call | tf_op jit(solution)/shard_map/pallas_call | solution.py:323
  42.9 0.7 %copy.22 = f32[128,2,256]{2,1,0:T(2,128)} copy(f32[128,2,256]{2,1,0:T(2,128)S(1)} %bitcast.17) | data formatting | bytes 524288
  43.6 0.6 %copy.23 = f32[2,8]{1,0:T(2,128)} copy(f32[2,8]{1,0:T(2,128)S(1)} %get-tuple-element.9) | data formatting | bytes 128
  (2 shorter events, 0.1 us)
Async XLA Ops:
  0.6 1.6 %copy-start = (bf16[4,1,80,2,1536]{4,3,2,1,0:T(2,128)(2,1)S(1)}, bf16[4,1,80,2,1536]{4,3,2,1,0:T(2,128)(2,1)}, u32[]{:S(2)}) copy-start(bf16[4,1,80,2,1536]{4,3,2,1,0:T(2,128)(2,1)} %param.9) | copy-start | bytes 5898244
  0.6 4.8 %copy-start.2 = (s32[128]{0:T(128)S(1)}, s32[128]{0:T(128)}, u32[]{:S(2)}) copy-start(s32[128]{0:T(128)} %param.16) | copy-start | bytes 1540
  0.7 4.6 %copy-start.4 = (s32[128]{0:T(128)S(1)}, s32[128]{0:T(128)}, u32[]{:S(2)}) copy-start(s32[128]{0:T(128)} %param.15) | copy-start | bytes 1540
  0.7 4.6 %copy-start.3 = (f32[128,256]{1,0:T(8,128)S(1)}, f32[128,256]{1,0:T(8,128)}, u32[]{:S(2)}) copy-start(f32[128,256]{1,0:T(8,128)} %param.14) | copy-start | bytes 393220
  0.7 4.7 %copy-start.1 = (bf16[128,10,256]{2,0,1:T(8,128)(2,1)S(1)}, bf16[128,10,256]{2,0,1:T(8,128)(2,1)}, u32[]{:S(2)}) copy-start(bf16[128,10,256]{2,0,1:T(8,128)(2,1)} %param.13) | copy-start | bytes 1966084

commit v2 on v0

v2 whole, which is shorter than its diff:
```python
import functools
import math

import jax
import jax.numpy as jnp
from jax import lax
from jax.experimental.layout import Layout, with_layout_constraint
from jax.experimental import pallas as pl
from jax.experimental.pallas import tpu as pltpu
from jax.sharding import Mesh
from jax.sharding import PartitionSpec as P

NLAT_GRID = 768
LAT0 = 256
REGIONS = 4
NTYPES = 8
LAT = ("lat_0", "lat_1", "lat_2")
MESH = pl.DeviceIdType.MESH
F32 = jnp.float32
BF16 = jnp.bfloat16


def ring_order(n):
    return sorted(range(1, n), key=lambda d: (-min(d, n - d), d))


def exchange_kernel(
    dims,
    counts,
    norm_scale,
    member_scale,
    total_scale,
    anom_ref,
    now_ref,
    prior_ref,
    energy_ref,
    obs_ref,
    innov_ref,
    valid_ref,
    type_ref,
    inverse_ref,
    out_ref,
    tot_ref,
    anom,
    now,
    prior,
    energy,
    obs,
    innov,
    valid,
    types,
    inverse,
    folded,
    scal,
    mz,
    my,
    mx,
    mz_src,
    my_src,
    mx_src,
    near,
    far_up,
    far_down,
    resp_src,
    resp_in,
    pt_src,
    pt_in,
    load_sem,
    mz_send,
    mz_recv,
    my_send,
    my_recv,
    mx_send,
    mx_recv,
    ob_send,
    ob_recv,
    rs_send,
    rs_recv,
    pt_send,
    pt_recv,
):
    nx, ny, nc, nz = dims
    variables, total_members, lat_rows = counts
    members, slots, rows = obs.shape
    owners = nz // 2
    block = slots // owners
    half = block // 2
    targets = variables * REGIONS
    pair = targets // nz
    lon_tiles = now.shape[1]
    xi = lax.axis_index("lat_0")
    yi = lax.axis_index("lat_1")
    ci = lax.axis_index("lat_2")
    zi = lax.axis_index("lev")

    def loads(pairs, first):
        copies = []
        for i, (a, b) in enumerate(pairs):
            copy = pltpu.make_async_copy(a, b, load_sem.at[first + i])
            copy.start()
            copies.append(copy)
        return copies

    grad_loads = loads([(now_ref, now), (prior_ref, prior), (energy_ref, energy)], 0)
    anom_loads = loads([(anom_ref.at[v], anom.at[v]) for v in range(variables)], 3)

    def z_peer(d):
        return {"lev": lax.rem(zi + d, nz)}

    def x_peer(d):
        return {"lat_0": lax.rem(xi + d, nx)}

    def y_peer(d, e):
        return {"lat_1": lax.rem(yi + d, ny), "lat_2": lax.rem(ci + e, nc)}

    def send(source, target, sems, d, peer):
        copy = pltpu.make_async_remote_copy(
            src_ref=source,
            dst_ref=target,
            send_sem=sems[0].at[d],
            recv_sem=sems[1].at[d],
            device_id=peer,
            device_id_type=MESH,
        )
        copy.start()
        return copy

    def iota(shape, axis):
        return lax.broadcasted_iota(jnp.int32, shape, axis)

    y_steps = [(d, e) for d in ring_order(ny) + [0] for e in range(nc) if d or e]
    barrier = pltpu.get_barrier_semaphore()
    peers = [z_peer(d) for d in ring_order(nz)]
    peers += [y_peer(d, e) for d, e in y_steps]
    peers += [x_peer(d) for d in ring_order(nx)]
    for peer in peers:
        pl.semaphore_signal(barrier, inc=1, device_id=peer, device_id_type=MESH)
    other_loads = loads(
        [
            (obs_ref, obs),
            (innov_ref, innov),
            (valid_ref, valid),
            (type_ref, types),
            (inverse_ref, inverse),
        ],
        3 + variables,
    )

    lat_index = ((xi * ny + yi) * nc + ci) * lat_rows + lax.rem(
        iota((lon_tiles, 128), 0), lat_rows
    )
    cosine = jnp.cos(
        -0.5 * math.pi + ((lat_index + LAT0).astype(F32) + 0.5) * math.pi / NLAT_GRID
    )
    for copy in grad_loads:
        copy.wait()
    spare = jnp.zeros((128 - total_members, 384), BF16)
    for v in range(variables):
        grad = energy[0:1, v : v + 1] * cosine * (now[v] + prior[v])
        grad = grad.astype(BF16).astype(F32)
        anom_loads[v].wait()
        step = 4
        for k in range(0, anom.shape[1], step):
            a = anom[v, k : k + step].astype(F32)
            a = a.reshape(-1, lon_tiles, 128) * grad[None]
            a = a.reshape(a.shape[0], lon_tiles // 8, 8, 128).sum(axis=1)
            folded[v, k * 16 : (k + step) * 16, :] = a.reshape(-1, 128)
    lines = []
    for v in range(variables):
        s = folded[v, pl.ds(0, total_members, stride=8), :]
        for r in range(1, 8):
            s = s + folded[v, pl.ds(r, total_members, stride=8), :]
        high = s.astype(BF16)
        rest = s - high.astype(F32)
        mid = rest.astype(BF16)
        low = (rest - mid.astype(F32)).astype(BF16)
        lines.append(
            jnp.concatenate([jnp.concatenate([high, mid, low], axis=1), spare], axis=0)
        )
    lanes_sum = lax.dot_general(
        jnp.ones((8, 384), BF16),
        jnp.concatenate(lines, axis=0),
        (((1,), (1,)), ((), ())),
        preferred_element_type=F32,
    )
    row4 = iota((4, 128), 0)
    lane4 = iota((4, 128), 1)
    base = jnp.zeros((4, 128), F32)
    for v in range(variables):
        base = jnp.where(row4 == v, lanes_sum[0:4, v * 128 : (v + 1) * 128], base)
    mz_src[0] = base
    mz[pl.ds(zi, 1)] = base[None]

    pl.semaphore_wait(barrier, len(peers))
    z_copies = [
        send(mz_src.at[0], mz.at[zi], (mz_send, mz_recv), d, z_peer(d))
        for d in ring_order(nz)
    ]

    for copy in other_loads:
        copy.wait()
    eye = iota((slots, slots), 0) == iota((slots, slots), 1)

    def column(line):
        wide = jnp.broadcast_to(line.astype(F32), (slots, slots))
        return jnp.sum(jnp.where(eye, wide, 0.0), axis=1, keepdims=True)

    type_col = column(types[...])
    valid_col = column(valid[...])
    inverse_col = jnp.zeros((slots, 1), F32)
    for c in range(NTYPES):
        inverse_col = jnp.where(type_col == c, inverse[0:1, c : c + 1], inverse_col)
    inside = iota((slots, rows), 1).astype(F32) < valid_col
    scaled = innov[...] * inverse_col * inside.astype(F32) / member_scale
    scal[...] = scaled
    onehot = (iota((NTYPES, slots), 0) == types[...]).astype(F32)
    g_add = jnp.zeros((4, 128), F32)
    for m in range(members):
        prod = obs[m].astype(F32) * scal[...]
        by_type = jnp.dot(
            onehot, prod, precision=lax.Precision.HIGHEST, preferred_element_type=F32
        )
        g = jnp.sum(by_type, axis=1, keepdims=True)
        g_add = jnp.where(lane4 == total_members + m, g[0:4], g_add)
        g_add = jnp.where(lane4 == total_members + members + m, g[4:8], g_add)
    my_class = lax.rem(zi, owners)
    mine = pl.ds(pl.multiple_of(my_class * block, block), block)
    near[1] = obs[:, mine, :]

    def select(cols, first):
        wanted = lax.rem(
            zi * members + (first * members + 2 * total_members) + iota((128, cols), 1) // half,
            total_members,
        )
        return (iota((128, cols), 0) == wanted).astype(BF16)

    one = members * half
    sel_near = select(3 * one, -1)
    sel_up = select(one, 2)
    sel_down = select(one, -2)
    row_t = iota((targets * half, targets), 0) // half
    spread = (
        iota((targets * half, targets), 1)
        == lax.rem(row_t, REGIONS) * variables + row_t // REGIONS
    ).astype(BF16)
    sel_own = (
        (iota((128, 128), 0) == iota((128, 128), 1) + zi * members)
        & (iota((128, 128), 1) < members)
    ).astype(BF16)
    perm_r = iota((targets, targets), 0)
    perm = (
        iota((targets, targets), 1) == lax.rem(perm_r, REGIONS) * variables + perm_r // REGIONS
    ).astype(BF16)

    for copy in z_copies:
        copy.wait()
    tot_z = mz[0]
    for z in range(1, nz):
        tot_z = tot_z + mz[z]
    tot_z = tot_z + g_add
    my_src[0] = tot_z
    here_y = yi * nc + ci
    my[pl.ds(here_y, 1)] = tot_z[None]
    y_copies = [
        send(my_src.at[0], my.at[here_y], (my_send, my_recv), d * nc + e, y_peer(d, e))
        for d, e in y_steps
    ]

    def class_at(d, first, size):
        c = lax.rem(zi + d, owners)
        return pl.ds(pl.multiple_of(c * block + first, half), size)

    sems = (ob_send, ob_recv)
    ob_copies = [
        send(obs.at[:, class_at(2, half, half), :], far_down, sems, 0, z_peer(2)),
        send(obs.at[:, class_at(nz - 2, 0, half), :], far_up, sems, 1, z_peer(nz - 2)),
        send(obs.at[:, class_at(1, 0, block), :], near.at[0], sems, 2, z_peer(1)),
        send(obs.at[:, class_at(nz - 1, 0, block), :], near.at[2], sems, 3, z_peer(nz - 1)),
    ]

    for copy in y_copies:
        copy.wait()
    tot_y = my[0]
    for y in range(1, ny * nc):
        tot_y = tot_y + my[y]
    mx_src[0] = tot_y
    mx[pl.ds(xi, 1)] = tot_y[None]
    x_copies = [
        send(mx_src.at[0], mx.at[xi], (mx_send, mx_recv), d, x_peer(d))
        for d in ring_order(nx)
    ]
    for copy in x_copies:
        copy.wait()

    sums = jnp.concatenate([mx[x] for x in range(nx)], axis=0)
    lane16 = iota((targets, 128), 1)
    w = jnp.where(lane16 < total_members, sums / norm_scale, 0.0).astype(BF16)
    g_all = mx[0]
    for x in range(1, nx):
        g_all = g_all + mx[x]

    def diagonal(sel):
        wide = jnp.dot(w, sel, preferred_element_type=F32).astype(BF16)
        tall = jnp.dot(spread, wide, preferred_element_type=F32)
        keep = lax.rem(iota(tall.shape, 0), half) == lax.rem(iota(tall.shape, 1), half)
        return jnp.where(keep, tall, 0.0).astype(BF16)

    wd_near = diagonal(sel_near)
    wd_up = diagonal(sel_up)
    wd_down = diagonal(sel_down)

    w_own = jnp.dot(w, sel_own, preferred_element_type=F32).astype(BF16)
    w_own = jnp.dot(perm, w_own, preferred_element_type=F32)
    g_rows = jnp.concatenate(
        [
            pltpu.roll(g_all, 128 - total_members, 1),
            pltpu.roll(g_all, 128 - total_members - members, 1),
        ],
        axis=0,
    )
    g_rows = jnp.where(iota((NTYPES, 128), 1) < members, g_rows, 0.0)
    share = jnp.zeros((targets, 128), F32)
    for c in range(NTYPES):
        col = jnp.sum(w_own * g_rows[c : c + 1], axis=1, keepdims=True)
        share = jnp.where(lane16 == c, col, share)
    for z in range(nz):
        pt_src[z, 0:pair, :] = share[pair * z : pair * z + pair]
    top = pl.ds(0, pair)
    pt_copies = [
        send(
            pt_src.at[lax.rem(zi + d, nz), top],
            pt_in.at[zi, top],
            (pt_send, pt_recv),
            d,
            z_peer(d),
        )
        for d in ring_order(nz)
    ]
    pt_in[pl.ds(zi, 1), 0:pair, :] = pt_src[pl.ds(zi, 1), 0:pair, :]

    for copy in ob_copies:
        copy.wait()
    rs_copies = []
    for g, (wd_far, far) in enumerate(((wd_up, far_up), (wd_down, far_down))):
        part = pl.ds(g * half, half)
        close = near[:, :, g * half : (g + 1) * half, :].reshape(3 * one, rows)
        answered = jnp.dot(wd_near, close, preferred_element_type=F32)
        answered += jnp.dot(
            wd_far, far[...].reshape(one, rows), preferred_element_type=F32
        )
        resp_src[:, g] = answered.astype(BF16).reshape(nz, pair, half, rows)
        for d in ring_order(nz):
            rs_copies.append(
                send(
                    resp_src.at[lax.rem(zi + d, nz), g],
                    resp_in.at[zi, g],
                    (rs_send, rs_recv),
                    g * nz + d,
                    z_peer(d),
                )
            )
    resp_in[pl.ds(zi, 1)] = resp_src[pl.ds(zi, 1)]

    for copy in rs_copies:
        copy.wait()
    for c in range(owners):
        for g in range(2):
            first = c * block + g * half
            for t in range(pair):
                value = resp_in[c, g, t].astype(F32) + resp_in[c + owners, g, t].astype(F32)
                value = value * scal[first : first + half, :]
                for lane in range(rows // 128):
                    place = (first * (rows // 128) + lane) * pair + t
                    out_ref[pl.ds(place, half, stride=pair * (rows // 128)), :] = value[
                        :, lane * 128 : (lane + 1) * 128
                    ]
    for copy in pt_copies:
        copy.wait()
    whole = pt_in[0, 0:pair, :]
    for z in range(1, nz):
        whole = whole + pt_in[z, 0:pair, :]
    tot_ref[...] = whole[:, 0:NTYPES] / total_scale


def local(
    anomalies,
    error_now,
    error_prior,
    energy_coef,
    obs_anomalies,
    innovations,
    valid_counts,
    type_ids,
    error_inverse,
):
    dims = tuple(lax.axis_size(a) for a in (*LAT, "lev"))
    nx, ny, nc, nz = dims
    variables, levels, members, lat_rows, lon_count = anomalies.shape
    slots, local_members, rows = obs_anomalies.shape
    lat_total = lat_rows * nx * ny * nc
    norm_scale = math.sqrt(levels * nz * lat_total * lon_count / REGIONS)
    member_scale = math.sqrt(members - 1)
    total_scale = math.sqrt(slots * nx * ny * nc * rows / NTYPES)
    targets = variables * REGIONS
    pair = targets // nz
    block = slots // (nz // 2)
    half = block // 2
    tiles = lon_count // 128 * lat_rows

    def by_tile(a):
        a = a.reshape(*a.shape[:-1], lon_count // 128, 128)
        n = a.ndim
        order = (*range(n - 3), n - 2, n - 3, n - 1)
        a = with_layout_constraint(a, Layout(major_to_minor=order))
        a = jnp.swapaxes(a, -3, -2)
        return a.reshape(*a.shape[:-3], tiles, 128)

    anom = by_tile(anomalies[:, 0]).reshape(variables, members // 2, 2 * tiles, 128)
    now = by_tile(error_now[:, 0])
    prior = by_tile(error_prior[:, 0])
    obs = jnp.transpose(obs_anomalies, (1, 0, 2))
    inputs = (
        anom,
        now,
        prior,
        energy_coef.reshape(1, variables),
        obs,
        innovations,
        valid_counts.reshape(1, slots),
        type_ids.reshape(1, slots),
        error_inverse.reshape(1, NTYPES),
    )
    vmem = pl.BlockSpec(memory_space=pltpu.VMEM)
    hbm = pl.BlockSpec(memory_space=pltpu.HBM)
    dma = pltpu.SemaphoreType.DMA
    table = pltpu.VMEM
    out, totals = pl.pallas_call(
        functools.partial(
            exchange_kernel,
            dims,
            (variables, members, lat_rows),
            norm_scale,
            member_scale,
            total_scale,
        ),
        out_shape=(
            jax.ShapeDtypeStruct((slots * pair * rows // 128, 128), F32),
            jax.ShapeDtypeStruct((pair, NTYPES), F32),
        ),
        in_specs=[hbm] * len(inputs),
        out_specs=(vmem, vmem),
        scratch_shapes=[table(a.shape, a.dtype) for a in inputs]
        + [
            table((variables, members * 8, 128), F32),
            table((slots, rows), F32),
            table((nz, 4, 128), F32),
            table((ny * nc, 4, 128), F32),
            table((nx, 4, 128), F32),
            table((1, 4, 128), F32),
            table((1, 4, 128), F32),
            table((1, 4, 128), F32),
            table((3, local_members, block, rows), BF16),
            table((local_members, half, rows), BF16),
            table((local_members, half, rows), BF16),
            table((nz, 2, pair, half, rows), BF16),
            table((nz, 2, pair, half, rows), BF16),
            table((nz, 8, 128), F32),
            table((nz, 8, 128), F32),
            dma((8 + variables,)),
            dma((nz,)),
            dma((nz,)),
            dma((ny * nc,)),
            dma((ny * nc,)),
            dma((nx,)),
            dma((nx,)),
            dma((4,)),
            dma((4,)),
            dma((2 * nz,)),
            dma((2 * nz,)),
            dma((nz,)),
            dma((nz,)),
        ],
        compiler_params=pltpu.CompilerParams(
            collective_id=0, has_side_effects=True, vmem_limit_bytes=24 * 1024 * 1024
        ),
    )(*inputs)
    impact = out.reshape(slots, rows // 128, pair, 128)
    impact = jnp.transpose(impact, (0, 2, 1, 3)).reshape(slots, pair, rows)
    return (impact, totals)


def solution(mesh):
    split = Mesh(
        mesh.devices.reshape(4, 8, 2, mesh.shape["lev"]), ("lat_0", "lat_1", "lat_2", "lev")
    )
    in_specs = (
        P(None, "lev", None, LAT, None),
        P(None, "lev", LAT, None),
        P(None, "lev", LAT, None),
        P(None, "lev"),
        P(LAT, "lev", None),
        P(LAT, None),
        P(LAT),
        P(LAT),
        P(),
    )
    out_specs = (P(LAT, "lev", None), P("lev", None))
    return jax.shard_map(local, mesh=split, in_specs=in_specs, out_specs=out_specs, check_vma=False)
```

time: 98.1 us -> 49 us (0.50)
  blocking collectives: 45.8 us -> 0 us
  Pallas kernels: 0 us -> 39 us
  starting transfers between devices: 25.4 us -> 0 us
  waiting for transfers between devices: 18 us -> 0 us
  local copies, waits for them, and re-layouts: 4.17 us -> 9.01 us
  other arithmetic: 2.21 us -> 0 us
  matrix products: 1.28 us -> 0 us
    psum x4 -> x0, blocking collectives: 45.8 us -> none  [over_axes(): return functools.reduce(lax.psum, axes, array)]
    pallas_call x0 -> x1, Pallas kernels: none -> 39 us  [local(): pl.pallas_call(functools.partial(exchange_kernel, dims, (variables, membe...]
    all_to_all x3 -> x0, starting transfers between devices: 25.4 us -> none  [the longest x1 10.9 us: local(): lax.all_to_all(grouped, 'lev', split_axis=0, concat_axis=2, tiled=True)]
    all_to_all x3 -> x0, waiting for transfers between devices: 18 us -> none  [the longest x1 9.03 us: local(): lax.all_to_all(answered[0], 'lev', split_axis=1, concat_axis=0, tiled=True)]
    unnamed x16 -> x20, local copies, waits for them, and re-layouts: 0.05 us -> 9.01 us
    reshape x1 -> x0, local copies, waits for them, and re-layouts: 2.12 us -> none  [local(): obs_anomalies.reshape(lev_groups, slot_count // lev_groups, local_members...]
    dot_general x4 -> x0, matrix products: 1.28 us -> none  [the longest x1 0.61 us: local(): jnp.einsum('vlkji,vlji->vkj', anomalies, gradient, preferred_element_type...]
  transfers between devices with their start and end apart: 3 -> 0, of which waited for: 2 -> 0; matrix products, arithmetic and copies ran while one was open for 2% -> 0% of each run, Pallas kernels for 0% -> 0%
where the time goes in v2:
time: 49 us; the launch traced here: 48.6 us
  Pallas kernels  39 us (80%)
  local copies, waits for them, and re-layouts  9.01 us (18%)
  between operations  0.66 us (1%)
    pallas_call x1, Pallas kernels, local(): pl.pallas_call(functools.partial(exchange_kernel, dims, (variables, membe...  39 us
    unnamed x20, local copies, waits for them, and re-layouts  9.01 us

profile of v2, /device:TPU:1, one launch (start us, length us, event | category | flops | bytes accessed | tf_op | source)
XLA Modules:
  0.0 48.6 jit_solution(6571576151009085506)
XLA Ops:
  0.6 0.0 copy-start
  0.6 1.5 %copy-done = bf16[4,1,80,2,1536]{4,3,2,1,0:T(2,128)(2,1)S(1)} copy-done((bf16[4,1,80,2,1536]{4,3,2,1,0:T(2,128)(2,1)S(1)}, bf16[4,1,80,2,1536]{4,3,2,1,0:T(2,128)(2,1)}, u32[]{:S(2)}) %copy-start) | copy-done | bytes 1966104
  2.2 0.0 copy-start.1
  2.2 1.1 %copy-done.1 = bf16[128,10,256]{2,0,1:T(8,128)(2,1)S(1)} copy-done((bf16[128,10,256]{2,0,1:T(8,128)(2,1)S(1)}, bf16[128,10,256]{2,0,1:T(8,128)(2,1)}, u32[]{:S(2)}) %copy-start.1) | copy-done | bytes 655384
  3.3 0.0 copy-start.2
  3.3 0.9 %copy-done.2 = f32[128,256]{1,0:T(8,128)S(1)} copy-done((f32[128,256]{1,0:T(8,128)S(1)}, f32[128,256]{1,0:T(8,128)}, u32[]{:S(2)}) %copy-start.2) | copy-done | bytes 131096
  4.2 0.0 copy-start.3
  4.2 0.8 %copy-done.3 = f32[4,1,2,1536]{3,2,1,0:T(2,128)S(1)} copy-done((f32[4,1,2,1536]{3,2,1,0:T(2,128)S(1)}, f32[4,1,2,1536]{3,2,1,0:T(2,128)}, u32[]{:S(2)}) %copy-start.3) | copy-done | bytes 49176
  5.0 0.0 copy-start.4
  5.0 0.8 %copy-done.4 = f32[4,1,2,1536]{3,2,1,0:T(2,128)S(1)} copy-done((f32[4,1,2,1536]{3,2,1,0:T(2,128)S(1)}, f32[4,1,2,1536]{3,2,1,0:T(2,128)}, u32[]{:S(2)}) %copy-start.4) | copy-done | bytes 49176
  5.8 0.0 copy-start.5
  5.8 0.7 %copy-done.5 = f32[4,1]{0,1:T(1,128)S(1)} copy-done((f32[4,1]{0,1:T(1,128)S(1)}, f32[4,1]{0,1:T(1,128)}, u32[]{:S(2)}) %copy-start.5) | copy-done | bytes 40
  6.4 0.0 copy-start.6
  6.4 0.7 %copy-done.6 = s32[128]{0:T(128)S(1)} copy-done((s32[128]{0:T(128)S(1)}, s32[128]{0:T(128)}, u32[]{:S(2)}) %copy-start.6) | copy-done | bytes 536
  7.1 0.0 copy-start.7
  7.1 0.7 %copy-done.7 = s32[128]{0:T(128)S(1)} copy-done((s32[128]{0:T(128)S(1)}, s32[128]{0:T(128)}, u32[]{:S(2)}) %copy-start.7) | copy-done | bytes 536
  7.7 0.0 copy-start.8
  7.7 0.7 %copy-done.8 = f32[8]{0:T(128)S(1)} copy-done((f32[8]{0:T(128)S(1)}, f32[8]{0:T(128)}, u32[]{:S(2)}) %copy-start.8) | copy-done | bytes 56
  8.4 39.0 %shard_map.104 = (f32[512,128]{1,0:T(8,128)S(1)}, f32[2,8]{1,0:T(2,128)S(1)}) custom-call(bf16[4,40,48,128]{3,2,1,0:T(8,128)(2,1)S(1)} %bitcast.25, f32[4,24,128]{2,1,0:T(8,128)S(1)} %bitcast.28, f32[4,24,128]{2,1,0:T(8,128)S(1)} %bitcast.29, f32[1,4]{1,0:T(1,128)S(1)} %bitcast.30, bf16[10,128,256]{2,1,0:T(8,128)(2,1)S(1)} %bitcast.26, ...), custom_call_target="tpu_custom_call" | custom-call | tf_op jit(solution)/shard_map/pallas_call | solution.py:437
  47.4 0.7 %copy.14 = f32[128,2,256]{2,1,0:T(2,128)} copy(f32[128,2,256]{2,1,0:T(2,128)S(1)} %bitcast.27) | data formatting | bytes 524288
  48.1 0.6 %copy.15 = f32[2,8]{1,0:T(2,128)} copy(f32[2,8]{1,0:T(2,128)S(1)} %get-tuple-element.9) | data formatting | bytes 128
Async XLA Ops:
  0.6 1.5 %copy-start = (bf16[4,1,80,2,1536]{4,3,2,1,0:T(2,128)(2,1)S(1)}, bf16[4,1,80,2,1536]{4,3,2,1,0:T(2,128)(2,1)}, u32[]{:S(2)}) copy-start(bf16[4,1,80,2,1536]{4,3,2,1,0:T(2,128)(2,1)} %param.9) | copy-start | bytes 5898244
  2.2 1.1 %copy-start.1 = (bf16[128,10,256]{2,0,1:T(8,128)(2,1)S(1)}, bf16[128,10,256]{2,0,1:T(8,128)(2,1)}, u32[]{:S(2)}) copy-start(bf16[128,10,256]{2,0,1:T(8,128)(2,1)} %param.13) | copy-start | bytes 1966084
  3.3 0.9 %copy-start.2 = (f32[128,256]{1,0:T(8,128)S(1)}, f32[128,256]{1,0:T(8,128)}, u32[]{:S(2)}) copy-start(f32[128,256]{1,0:T(8,128)} %innov_ref.1) | copy-start | bytes 393220
  4.2 0.8 %copy-start.3 = (f32[4,1,2,1536]{3,2,1,0:T(2,128)S(1)}, f32[4,1,2,1536]{3,2,1,0:T(2,128)}, u32[]{:S(2)}) copy-start(f32[4,1,2,1536]{3,2,1,0:T(2,128)} %param.10) | copy-start | bytes 147460
  5.0 0.8 %copy-start.4 = (f32[4,1,2,1536]{3,2,1,0:T(2,128)S(1)}, f32[4,1,2,1536]{3,2,1,0:T(2,128)}, u32[]{:S(2)}) copy-start(f32[4,1,2,1536]{3,2,1,0:T(2,128)} %param.11) | copy-start | bytes 147460
  5.8 0.7 %copy-start.5 = (f32[4,1]{0,1:T(1,128)S(1)}, f32[4,1]{0,1:T(1,128)}, u32[]{:S(2)}) copy-start(f32[4,1]{0,1:T(1,128)} %param.12) | copy-start | bytes 52
  6.4 0.7 %copy-start.6 = (s32[128]{0:T(128)S(1)}, s32[128]{0:T(128)}, u32[]{:S(2)}) copy-start(s32[128]{0:T(128)} %param.15) | copy-start | bytes 1540
  7.1 0.7 %copy-start.7 = (s32[128]{0:T(128)S(1)}, s32[128]{0:T(128)}, u32[]{:S(2)}) copy-start(s32[128]{0:T(128)} %param.16) | copy-start | bytes 1540
  7.7 0.7 %copy-start.8 = (f32[8]{0:T(128)S(1)}, f32[8]{0:T(128)}, u32[]{:S(2)}) copy-start(f32[8]{0:T(128)} %param.17) | copy-start | bytes 100

commit v3 on v2

--- a/solution.py
+++ b/solution.py
@@ -483,7 +483,7 @@
         compiler_params=pltpu.CompilerParams(
             collective_id=0, has_side_effects=True, vmem_limit_bytes=24 * 1024 * 1024
         ),
-    )(*inputs)
+    )(*(pltpu.with_memory_space_constraint(a, pltpu.HBM) for a in inputs))
     impact = out.reshape(slots, rows // 128, pair, 128)
     impact = jnp.transpose(impact, (0, 2, 1, 3)).reshape(slots, pair, rows)
     return (impact, totals)

time: 49 us -> 39.6 us (0.81)
  local copies, waits for them, and re-layouts: 9.01 us -> 1.27 us
  Pallas kernels: 39 us -> 37.5 us
    unnamed x20 -> x2, local copies, waits for them, and re-layouts: 9.01 us -> 1.27 us
    pallas_call x1, Pallas kernels: 39 us -> 37.5 us  [local(): pl.pallas_call(functools.partial(exchange_kernel, dims, (variables, membe...]
where the time goes in v3:
time: 39.6 us; the launch traced here: 39.4 us
  Pallas kernels  37.5 us (95%)
  local copies, waits for them, and re-layouts  1.27 us (3%)
  between operations  0.64 us (2%)
    pallas_call x1, Pallas kernels, local(): pl.pallas_call(functools.partial(exchange_kernel, dims, (variables, membe...  37.5 us
    unnamed x2, local copies, waits for them, and re-layouts  1.27 us

profile of v3, /device:TPU:1, one launch (start us, length us, event | category | flops | bytes accessed | tf_op | source)
XLA Modules:
  0.0 39.4 jit_solution(4590294276402203673)
XLA Ops:
  0.6 37.5 %shard_map.104 = (f32[512,128]{1,0:T(8,128)S(1)}, f32[2,8]{1,0:T(2,128)S(1)}) custom-call(bf16[4,40,48,128]{3,2,1,0:T(8,128)(2,1)} %bitcast.26, f32[4,24,128]{2,1,0:T(8,128)} %bitcast.28, f32[4,24,128]{2,1,0:T(8,128)} %bitcast.29, f32[1,4]{1,0:T(1,128)} %bitcast.30, bf16[10,128,256]{2,1,0:T(8,128)(2,1)} %bitcast.27, f32[128,256]{1,0:T(8,128)} %innov_ref.1, ...), custom_call_target="tpu_custom_call" | custom-call | tf_op jit(solution)/shard_map/pallas_call | solution.py:437
  38.2 0.7 %copy.14 = f32[128,2,256]{2,1,0:T(2,128)} copy(f32[128,2,256]{2,1,0:T(2,128)S(1)} %bitcast.25) | data formatting | bytes 524288
  38.9 0.6 %copy.15 = f32[2,8]{1,0:T(2,128)} copy(f32[2,8]{1,0:T(2,128)S(1)} %get-tuple-element.9) | data formatting | bytes 128

commit v4 on v3

v4 whole, which is shorter than its diff:
```python
import functools
import math

import jax
import jax.numpy as jnp
from jax import lax
from jax.experimental.layout import Layout, with_layout_constraint
from jax.experimental import pallas as pl
from jax.experimental.pallas import tpu as pltpu
from jax.sharding import Mesh
from jax.sharding import PartitionSpec as P

NLAT_GRID = 768
LAT0 = 256
REGIONS = 4
NTYPES = 8
LAT = ("lat_0", "lat_1", "lat_2")
MESH = pl.DeviceIdType.MESH
EARLY = True
SHARES = (1, 1, 1)
F32 = jnp.float32
BF16 = jnp.bfloat16


def ring_order(n):
    return sorted(range(1, n), key=lambda d: (-min(d, n - d), d))


def exchange_kernel(
    dims,
    counts,
    shares,
    norm_scale,
    member_scale,
    total_scale,
    anom_ref,
    now_ref,
    prior_ref,
    energy_ref,
    obs_ref,
    innov_ref,
    valid_ref,
    type_ref,
    inverse_ref,
    out_ref,
    tot_ref,
    anom,
    errors,
    energy,
    obs,
    innov,
    valid,
    types,
    inverse,
    folded,
    scal,
    mz,
    my,
    mx,
    sums_src,
    g_in,
    near,
    far_up,
    far_down,
    single,
    packed,
    packed_single,
    resp_src,
    resp_in,
    pt_src,
    pt_in,
    load_sem,
    mz_sem,
    g_sem,
    my_sem,
    mx_sem,
    ob_sem,
    rs_sem,
    pt_sem,
):
    nx, ny, nc, nz = dims
    variables, total_members, lat_rows = counts
    n_up, n_down, n_single = shares
    groups, members, eight, rows = obs.shape
    slots = groups * eight
    owners = nz // 2
    double = n_up + n_down
    single_base = owners * double
    pieces = double + n_single
    targets = variables * REGIONS
    pair = targets // nz
    lon_tiles = errors.shape[2]
    one = members * eight
    xi = lax.axis_index("lat_0")
    yi = lax.axis_index("lat_1")
    ci = lax.axis_index("lat_2")
    zi = lax.axis_index("lev")
    lead = nc - 1

    def z_peer(d, core=None):
        peer = {"lev": lax.rem(zi + d, nz)}
        if core is not None:
            peer["lat_2"] = core
        return peer

    def x_peer(d, core=None):
        peer = {"lat_0": lax.rem(xi + d, nx)}
        if core is not None:
            peer["lat_2"] = core
        return peer

    def y_peer(d):
        return {"lat_1": lax.rem(yi + d, ny)}

    def remote(source, target, send_sem, recv_sem, peer):
        return pltpu.make_async_remote_copy(
            src_ref=source,
            dst_ref=target,
            send_sem=send_sem,
            recv_sem=recv_sem,
            device_id=peer,
            device_id_type=MESH,
        )

    def send(source, target, send_sem, recv_sem, peer):
        remote(source, target, send_sem, recv_sem, peer).start()

    def iota(shape, axis):
        return lax.broadcasted_iota(jnp.int32, shape, axis)

    barrier = pltpu.get_barrier_semaphore()
    other_core = nc - 1 - ci
    partner = {"lat_2": other_core}

    def greet(hops):
        for _, peer in sorted(hops, key=lambda h: -h[0]):
            pl.semaphore_signal(barrier, inc=1, device_id=peer, device_id_type=MESH)

    def far(d, n):
        return min(d, n - d)

    z_same = [(far(d, nz), z_peer(d)) for d in ring_order(nz)]
    x_lead = [(far(d, nx), x_peer(d, lead)) for d in ring_order(nx)]

    @pl.when(ci == lead)
    def _():
        z_other = [(far(d, nz), z_peer(d, other_core)) for d in ring_order(nz)]
        along_y = [(far(d, ny), y_peer(d)) for d in ring_order(ny)]
        greet(z_same + z_other + along_y + x_lead + [(0, partner)])

    @pl.when(ci != lead)
    def _():
        greet(z_same + x_lead + [(0, partner)])

    def load(source, target, n):
        pltpu.make_async_copy(source, target, load_sem.at[n]).start()

    def landed(target, sem):
        pltpu.make_async_copy(target, target, sem).wait()

    load(now_ref, errors.at[0], 0)
    load(prior_ref, errors.at[1], 0)
    load(energy_ref, energy, 1)
    for v in range(variables):
        load(anom_ref.at[v], anom.at[v], 6 + v)
    for m in range(members):
        load(obs_ref.at[m], obs.at[:, m], 6 + variables)
    load(innov_ref, innov, 2)
    load(valid_ref, valid, 3)
    load(type_ref, types, 4)
    load(inverse_ref, inverse, 5)

    lat_index = ((xi * ny + yi) * nc + ci) * lat_rows + lax.rem(
        iota((lon_tiles, 128), 0), lat_rows
    )
    cosine = jnp.cos(
        -0.5 * math.pi + ((lat_index + LAT0).astype(F32) + 0.5) * math.pi / NLAT_GRID
    )
    landed(errors, load_sem.at[0])
    landed(energy, load_sem.at[1])
    spare = jnp.zeros((128 - total_members, 384), BF16)
    for v in range(variables):
        grad = energy[0:1, v : v + 1] * cosine * (errors[0, v] + errors[1, v])
        grad = grad.astype(BF16).astype(F32)
        landed(anom.at[v], load_sem.at[6 + v])
        step = 4
        for k in range(0, anom.shape[1], step):
            a = anom[v, k : k + step].astype(F32)
            a = a.reshape(-1, lon_tiles, 128) * grad[None]
            a = a.reshape(a.shape[0], lon_tiles // 8, 8, 128).sum(axis=1)
            folded[v, k * 16 : (k + step) * 16, :] = a.reshape(-1, 128)
    lines = []
    for v in range(variables):
        s = folded[v, pl.ds(0, total_members, stride=8), :]
        for r in range(1, 8):
            s = s + folded[v, pl.ds(r, total_members, stride=8), :]
        high = s.astype(BF16)
        rest = s - high.astype(F32)
        mid = rest.astype(BF16)
        low = (rest - mid.astype(F32)).astype(BF16)
        lines.append(
            jnp.concatenate([jnp.concatenate([high, mid, low], axis=1), spare], axis=0)
        )
    lanes_sum = lax.dot_general(
        jnp.ones((8, 384), BF16),
        jnp.concatenate(lines, axis=0),
        (((1,), (1,)), ((), ())),
        preferred_element_type=F32,
    )
    row4 = iota((4, 128), 0)
    lane4 = iota((4, 128), 1)
    base = jnp.zeros((4, 128), F32)
    for v in range(variables):
        base = jnp.where(row4 == v, lanes_sum[0:4, v * 128 : (v + 1) * 128], base)
    sums_src[0] = base
    here_z = zi * nc + ci
    mz[pl.ds(here_z, 1)] = base[None]

    def z_copy(d):
        return remote(
            sums_src.at[0],
            mz.at[here_z],
            mz_sem.at[0],
            mz_sem.at[1],
            z_peer(d, lead),
        )

    @pl.when(ci == lead)
    def _():
        pl.semaphore_wait(barrier, nz - 1 + ny - 1 + nc * (nx - 1) + 1)

    @pl.when(ci != lead)
    def _():
        pl.semaphore_wait(barrier, nc * (nz - 1) + 1)

    for d in ring_order(nz):
        z_copy(d).start()

    @pl.when(ci != lead)
    def _():
        z_copy(0).start()

    def obs_copies():
        def double_at(d, first, size):
            c = lax.rem(zi + d, owners)
            return pl.ds(c * double + first, size)

        far = nz - 2
        send(obs.at[double_at(2, n_up, n_down)], far_down, ob_sem.at[0], ob_sem.at[1], z_peer(2))
        send(obs.at[double_at(far, 0, n_up)], far_up, ob_sem.at[2], ob_sem.at[3], z_peer(far))
        if n_single:
            for d in ring_order(nz):
                there = pl.ds(single_base + lax.rem(zi + d, nz) * n_single, n_single)
                send(obs.at[there], single.at[zi], ob_sem.at[6], ob_sem.at[7], z_peer(d))
        for d, slot in ((1, 0), (nz - 1, 2)):
            source = obs.at[double_at(d, 0, double)]
            send(source, near.at[slot], ob_sem.at[4], ob_sem.at[5], z_peer(d))

    landed(obs, load_sem.at[6 + variables])
    if EARLY:
        obs_copies()

    landed(innov, load_sem.at[2])
    landed(valid, load_sem.at[3])
    landed(types, load_sem.at[4])
    landed(inverse, load_sem.at[5])
    eye = iota((slots, slots), 0) == iota((slots, slots), 1)

    def column(line):
        wide = jnp.broadcast_to(line.astype(F32), (slots, slots))
        return jnp.sum(jnp.where(eye, wide, 0.0), axis=1, keepdims=True)

    type_col = column(types[...])
    valid_col = column(valid[...])
    inverse_col = jnp.zeros((slots, 1), F32)
    for c in range(NTYPES):
        inverse_col = jnp.where(type_col == c, inverse[0:1, c : c + 1], inverse_col)
    inside = iota((slots, rows), 1).astype(F32) < valid_col
    scal[...] = innov[...] * inverse_col * inside.astype(F32) / member_scale
    onehot = (iota((NTYPES, slots), 0) == types[...]).astype(BF16)
    onehot = jnp.concatenate([onehot, onehot], axis=1)
    g_add = jnp.zeros((4, 128), F32)
    for m in range(members):
        prod = obs[:, m].astype(F32).reshape(slots, rows) * scal[...]
        high = prod.astype(BF16)
        low = (prod - high.astype(F32)).astype(BF16)
        by_type = jnp.dot(
            onehot, jnp.concatenate([high, low], axis=0), preferred_element_type=F32
        )
        g = jnp.sum(by_type, axis=1, keepdims=True)
        g_add = jnp.where(lane4 == total_members + m, g[0:4], g_add)
        g_add = jnp.where(lane4 == total_members + members + m, g[4:8], g_add)
    sums_src[1] = g_add

    def g_copy():
        return remote(
            sums_src.at[1], g_in.at[0], g_sem.at[0], g_sem.at[1], {"lat_2": other_core}
        )

    @pl.when(ci != lead)
    def _():
        g_copy().start()

    my_class = lax.rem(zi, owners)
    near[1] = obs[pl.ds(my_class * double, double)]
    if n_single:
        single[pl.ds(zi, 1)] = obs[pl.ds(single_base + zi * n_single, n_single)][None]

    width = 4 * one
    pitch = -(-width // 128) * 128
    spot = iota((128, pitch), 1)

    def select(first):
        wanted = lax.rem(
            (zi + nz + first) * members + spot // eight, total_members
        )
        return ((iota((128, pitch), 0) == wanted) & (spot < width)).astype(BF16)

    tables = [select(-1), select(-2)]
    if n_single:
        shape = (128, nz * one)
        tables.append((iota(shape, 0) == iota(shape, 1) // eight).astype(BF16))
    sel = jnp.concatenate(tables, axis=1)
    row_t = iota((targets * eight, targets), 0) // eight
    spread = (
        iota((targets * eight, targets), 1)
        == lax.rem(row_t, REGIONS) * variables + row_t // REGIONS
    ).astype(BF16)
    sel_own = (
        (iota((128, 128), 0) == iota((128, 128), 1) + zi * members)
        & (iota((128, 128), 1) < members)
    ).astype(BF16)
    perm_r = iota((targets, targets), 0)
    perm = (
        iota((targets, targets), 1) == lax.rem(perm_r, REGIONS) * variables + perm_r // REGIONS
    ).astype(BF16)

    def y_copy(d):
        return remote(
            sums_src.at[2], my.at[yi], my_sem.at[0], my_sem.at[1], y_peer(d)
        )

    def x_copy(d, core):
        return remote(
            sums_src.at[3],
            mx.at[xi],
            mx_sem.at[0],
            mx_sem.at[1],
            x_peer(d, core),
        )

    @pl.when(ci == lead)
    def _():
        g_copy().wait_recv()
        landed(mz.at[pl.ds(0, nz * nc - 1)], mz_sem.at[1])
        total = mz[0]
        for z in range(1, nz * nc):
            total = total + mz[z]
        total = total + g_add + g_in[0]
        sums_src[2] = total
        my[pl.ds(yi, 1)] = total[None]
        for d in ring_order(ny):
            y_copy(d).start()

    if not EARLY:
        obs_copies()

    @pl.when(ci == lead)
    def _():
        landed(my.at[pl.ds(0, ny - 1)], my_sem.at[1])
        total = my[0]
        for y in range(1, ny):
            total = total + my[y]
        sums_src[3] = total
        mx[pl.ds(xi, 1)] = total[None]
        for d in ring_order(nx) + [0]:
            for core in range(nc):
                if d or core != lead:
                    x_copy(d, core).start()

    landed(far_down, ob_sem.at[1])
    landed(far_up, ob_sem.at[3])
    landed(near.at[pl.ds(0, 2)], ob_sem.at[5])
    if n_single:
        landed(single.at[pl.ds(0, nz - 1)], ob_sem.at[7])

    def rows_of(value):
        return value.astype(F32).reshape(-1, rows).astype(BF16)

    for p in range(double):
        close = rows_of(near[:, p])
        if p < n_up:
            packed[p, 0 : 3 * one, :] = close
            packed[p, 3 * one : width, :] = rows_of(far_up[p])
        else:
            packed[p, one:width, :] = close
            packed[p, 0:one, :] = rows_of(far_down[p - n_up])
    for p in range(n_single):
        packed_single[p] = rows_of(single[:, p])

    @pl.when(ci == lead)
    def _():
        landed(mx.at[pl.ds(0, nx - 1)], mx_sem.at[1])

    @pl.when(ci != lead)
    def _():
        landed(mx, mx_sem.at[1])

    sums = jnp.concatenate([mx[x] for x in range(nx)], axis=0)
    lane16 = iota((targets, 128), 1)
    w = jnp.where(lane16 < total_members, sums / norm_scale, 0.0).astype(BF16)
    wide = jnp.dot(w, sel, preferred_element_type=F32).astype(BF16)
    tall = jnp.dot(spread, wide, preferred_element_type=F32)
    keep = lax.rem(iota(tall.shape, 0), eight) == lax.rem(iota(tall.shape, 1), eight)
    wd = jnp.where(keep, tall, 0.0).astype(BF16)

    for p in range(pieces):
        if p < double:
            first = 0 if p < n_up else pitch
            answered = jnp.dot(
                wd[:, first : first + width], packed[p], preferred_element_type=F32
            )
        else:
            answered = jnp.dot(
                wd[:, 2 * pitch :], packed_single[p - double], preferred_element_type=F32
            )
        resp_src[:, p] = answered.astype(BF16).reshape(nz, pair * eight, rows)
        for d in ring_order(nz):
            send(
                resp_src.at[lax.rem(zi + d, nz), p],
                resp_in.at[zi, p],
                rs_sem.at[pieces],
                rs_sem.at[p],
                z_peer(d),
            )

    g_all = mx[0]
    for x in range(1, nx):
        g_all = g_all + mx[x]
    w_own = jnp.dot(w, sel_own, preferred_element_type=F32).astype(BF16)
    w_own = jnp.dot(perm, w_own, preferred_element_type=F32)
    g_rows = jnp.concatenate(
        [
            pltpu.roll(g_all, 128 - total_members, 1),
            pltpu.roll(g_all, 128 - total_members - members, 1),
        ],
        axis=0,
    )
    g_rows = jnp.where(iota((NTYPES, 128), 1) < members, g_rows, 0.0)
    share = jnp.zeros((targets, 128), F32)
    for c in range(NTYPES):
        col = jnp.sum(w_own * g_rows[c : c + 1], axis=1, keepdims=True)
        share = jnp.where(lane16 == c, col, share)
    for z in range(nz):
        pt_src[z, 0:pair, :] = share[pair * z : pair * z + pair]
    top = pl.ds(0, pair)
    for d in ring_order(nz):
        other = lax.rem(zi + d, nz)
        send(pt_src.at[other, top], pt_in.at[zi, top], pt_sem.at[0], pt_sem.at[1], z_peer(d))
    pt_in[pl.ds(zi, 1), 0:pair, :] = pt_src[pl.ds(zi, 1), 0:pair, :]
    resp_in[pl.ds(zi, 1)] = resp_src[pl.ds(zi, 1)]

    def place(value, group):
        start = group * eight
        for t in range(pair):
            line = value[t * eight : (t + 1) * eight] * scal[start : start + eight, :]
            for lane in range(rows // 128):
                spot = (start * (rows // 128) + lane) * pair + t
                out_ref[pl.ds(spot, eight, stride=pair * (rows // 128)), :] = line[
                    :, lane * 128 : (lane + 1) * 128
                ]

    for p in range(pieces):
        landed(resp_in.at[pl.ds(0, nz - 1), p], rs_sem.at[p])
        if p < double:
            for c in range(owners):
                value = resp_in[c, p].astype(F32) + resp_in[c + owners, p].astype(F32)
                place(value, c * double + p)
        else:
            for z in range(nz):
                place(resp_in[z, p].astype(F32), single_base + z * n_single + p - double)
    landed(pt_in.at[pl.ds(0, nz - 1), top], pt_sem.at[1])
    whole = pt_in[0, 0:pair, :]
    for z in range(1, nz):
        whole = whole + pt_in[z, 0:pair, :]
    tot_ref[...] = whole[:, 0:NTYPES] / total_scale

    landed(far_down, ob_sem.at[0])
    landed(far_up, ob_sem.at[2])
    landed(near.at[pl.ds(0, 2)], ob_sem.at[4])
    if n_single:
        landed(single.at[pl.ds(0, nz - 1)], ob_sem.at[6])
    landed(resp_src.at[pl.ds(0, nz - 1)], rs_sem.at[pieces])
    landed(pt_src.at[pl.ds(0, nz - 1), top], pt_sem.at[0])

    @pl.when(ci != lead)
    def _():
        landed(mz.at[pl.ds(0, nz)], mz_sem.at[0])
        g_copy().wait_send()

    @pl.when(ci == lead)
    def _():
        landed(mz.at[pl.ds(0, nz - 1)], mz_sem.at[0])
        landed(my.at[pl.ds(0, ny - 1)], my_sem.at[0])
        landed(mz.at[pl.ds(0, nx * nc - 1)], mx_sem.at[0])


def store_kernel(out_ref, tot_ref, out_hbm, tot_hbm, sems):
    copies = [
        pltpu.make_async_copy(out_ref, out_hbm, sems.at[0]),
        pltpu.make_async_copy(tot_ref, tot_hbm, sems.at[1]),
    ]
    for copy in copies:
        copy.start()
    for copy in copies:
        copy.wait()


def local(
    anomalies,
    error_now,
    error_prior,
    energy_coef,
    obs_anomalies,
    innovations,
    valid_counts,
    type_ids,
    error_inverse,
):
    dims = tuple(lax.axis_size(a) for a in (*LAT, "lev"))
    nx, ny, nc, nz = dims
    variables, levels, members, lat_rows, lon_count = anomalies.shape
    slots, local_members, rows = obs_anomalies.shape
    lat_total = lat_rows * nx * ny * nc
    norm_scale = math.sqrt(levels * nz * lat_total * lon_count / REGIONS)
    member_scale = math.sqrt(members - 1)
    total_scale = math.sqrt(slots * nx * ny * nc * rows / NTYPES)
    targets = variables * REGIONS
    pair = targets // nz
    n_up, n_down, n_single = SHARES
    double = n_up + n_down
    pieces = double + n_single
    tiles = lon_count // 128 * lat_rows

    def by_tile(a):
        a = a.reshape(*a.shape[:-1], lon_count // 128, 128)
        n = a.ndim
        order = (*range(n - 3), n - 2, n - 3, n - 1)
        a = with_layout_constraint(a, Layout(major_to_minor=order))
        a = jnp.swapaxes(a, -3, -2)
        return a.reshape(*a.shape[:-3], tiles, 128)

    anom = by_tile(anomalies[:, 0]).reshape(variables, members // 2, 2 * tiles, 128)
    now = by_tile(error_now[:, 0])
    prior = by_tile(error_prior[:, 0])
    obs = jnp.transpose(obs_anomalies, (1, 0, 2)).reshape(local_members, slots // 8, 8, rows)
    inputs = (
        anom,
        now,
        prior,
        energy_coef.reshape(1, variables),
        obs,
        innovations,
        valid_counts.reshape(1, slots),
        type_ids.reshape(1, slots),
        error_inverse.reshape(1, NTYPES),
    )
    vmem = pl.BlockSpec(memory_space=pltpu.VMEM)
    hbm = pl.BlockSpec(memory_space=pltpu.HBM)
    dma = pltpu.SemaphoreType.DMA
    table = pltpu.VMEM
    out, totals = pl.pallas_call(
        functools.partial(
            exchange_kernel,
            dims,
            (variables, members, lat_rows),
            SHARES,
            norm_scale,
            member_scale,
            total_scale,
        ),
        out_shape=(
            jax.ShapeDtypeStruct((slots * pair * rows // 128, 128), F32),
            jax.ShapeDtypeStruct((pair, NTYPES), F32),
        ),
        in_specs=[hbm] * len(inputs),
        out_specs=(vmem, vmem),
        scratch_shapes=[
            table(anom.shape, BF16),
            table((2, *now.shape), F32),
            table((1, variables), F32),
            table((slots // 8, local_members, 8, rows), BF16),
            table((slots, rows), F32),
            table((1, slots), jnp.int32),
            table((1, slots), jnp.int32),
            table((1, NTYPES), F32),
        ]
        + [
            table((variables, members * 8, 128), F32),
            table((slots, rows), F32),
            table((nz * nc, 4, 128), F32),
            table((ny, 4, 128), F32),
            table((nx, 4, 128), F32),
            table((4, 4, 128), F32),
            table((1, 4, 128), F32),
            table((3, double, local_members, 8, rows), BF16),
            table((n_up, local_members, 8, rows), BF16),
            table((n_down, local_members, 8, rows), BF16),
            table((nz, max(n_single, 1), local_members, 8, rows), BF16),
            table((double, 32 * local_members, rows), BF16),
            table((max(n_single, 1), 8 * nz * local_members, rows), BF16),
            table((nz, pieces, pair * 8, rows), BF16),
            table((nz, pieces, pair * 8, rows), BF16),
            table((nz, 8, 128), F32),
            table((nz, 8, 128), F32),
            dma((7 + variables,)),
            dma((2,)),
            dma((2,)),
            dma((2,)),
            dma((2,)),
            dma((8,)),
            dma((pieces + 1,)),
            dma((2,)),
        ],
        compiler_params=pltpu.CompilerParams(
            collective_id=0, has_side_effects=True, vmem_limit_bytes=24 * 1024 * 1024
        ),
    )(*(pltpu.with_memory_space_constraint(a, pltpu.HBM) for a in inputs))
    out, totals = pl.pallas_call(
        store_kernel,
        out_shape=(pltpu.HBM(out.shape, F32), pltpu.HBM(totals.shape, F32)),
        in_specs=[vmem, vmem],
        out_specs=(hbm, hbm),
        scratch_shapes=[dma((2,))],
        compiler_params=pltpu.CompilerParams(vmem_limit_bytes=4 * 1024 * 1024),
    )(out, totals)
    impact = out.reshape(slots, rows // 128, pair, 128)
    impact = jnp.transpose(impact, (0, 2, 1, 3)).reshape(slots, pair, rows)
    return (impact, totals)


def solution(mesh):
    split = Mesh(
        mesh.devices.reshape(4, 8, 2, mesh.shape["lev"]), ("lat_0", "lat_1", "lat_2", "lev")
    )
    in_specs = (
        P(None, "lev", None, LAT, None),
        P(None, "lev", LAT, None),
        P(None, "lev", LAT, None),
        P(None, "lev"),
        P(LAT, "lev", None),
        P(LAT, None),
        P(LAT),
        P(LAT),
        P(),
    )
    out_specs = (P(LAT, "lev", None), P("lev", None))
    return jax.shard_map(local, mesh=split, in_specs=in_specs, out_specs=out_specs, check_vma=False)
```

time: 39.6 us -> 36.6 us (0.924)
  Pallas kernels: 37.5 us -> 35.8 us
  local copies, waits for them, and re-layouts: 1.27 us -> 0 us
    pallas_call x1, Pallas kernels: 37.5 us -> 35.1 us  [local(): pl.pallas_call(functools.partial(exchange_kernel, dims, (variables, membe...]
    unnamed x2 -> x0, local copies, waits for them, and re-layouts: 1.27 us -> none
    pallas_call x0 -> x1, Pallas kernels: none -> 0.72 us  [local(): pl.pallas_call(store_kernel, out_shape=(pltpu.HBM(out.shape, F32), pltpu....]
where the time goes in v4:
time: 36.6 us; the launch traced here: 36.5 us
  Pallas kernels  35.8 us (98%)
  between operations  0.64 us (2%)
    pallas_call x1, Pallas kernels, local(): pl.pallas_call(functools.partial(exchange_kernel, dims, (variables, membe...  35.1 us

profile of v4, /device:TPU:1, one launch (start us, length us, event | category | flops | bytes accessed | tf_op | source)
XLA Modules:
  0.0 36.5 jit_solution(2906550325791326869)
XLA Ops:
  0.6 35.1 %shard_map.104 = (f32[512,128]{1,0:T(8,128)S(1)}, f32[2,8]{1,0:T(2,128)S(1)}) custom-call(bf16[4,40,48,128]{3,2,1,0:T(8,128)(2,1)} %bitcast.27, f32[4,24,128]{2,1,0:T(8,128)} %bitcast.29, f32[4,24,128]{2,1,0:T(8,128)} %bitcast.30, f32[1,4]{1,0:T(1,128)} %bitcast.31, bf16[10,16,8,256]{3,2,1,0:T(8,128)(2,1)} %bitcast.28, f32[128,256]{1,0:T(8,128)} %innov_ref.1, ...), custom_call_target="tpu_custom_call" | custom-call | tf_op jit(solution)/shard_map/pallas_call | solution.py:572
  35.7 0.7 %shard_map.105 = (f32[512,128]{1,0:T(8,128)}, f32[2,8]{1,0:T(2,128)}) custom-call(f32[512,128]{1,0:T(8,128)S(1)} %get-tuple-element.6.out_ref, f32[2,8]{1,0:T(2,128)S(1)} %get-tuple-element.7.tot_ref), custom_call_target="tpu_custom_call" | custom-call | tf_op jit(solution)/shard_map/pallas_call | solution.py:629

commit v5 on v4

--- a/solution.py
+++ b/solution.py
@@ -17,7 +17,7 @@
 LAT = ("lat_0", "lat_1", "lat_2")
 MESH = pl.DeviceIdType.MESH
 EARLY = True
-SHARES = (1, 1, 1)
+SHARES = (2, 0, 1)
 F32 = jnp.float32
 BF16 = jnp.bfloat16
 
@@ -178,7 +178,6 @@
     )
     landed(errors, load_sem.at[0])
     landed(energy, load_sem.at[1])
-    spare = jnp.zeros((128 - total_members, 384), BF16)
     for v in range(variables):
         grad = energy[0:1, v : v + 1] * cosine * (errors[0, v] + errors[1, v])
         grad = grad.astype(BF16).astype(F32)
@@ -189,29 +188,16 @@
             a = a.reshape(-1, lon_tiles, 128) * grad[None]
             a = a.reshape(a.shape[0], lon_tiles // 8, 8, 128).sum(axis=1)
             folded[v, k * 16 : (k + step) * 16, :] = a.reshape(-1, 128)
-    lines = []
+    lane80 = iota((total_members, 128), 1)
+    flat = jnp.zeros((total_members, 128), F32)
     for v in range(variables):
         s = folded[v, pl.ds(0, total_members, stride=8), :]
         for r in range(1, 8):
             s = s + folded[v, pl.ds(r, total_members, stride=8), :]
-        high = s.astype(BF16)
-        rest = s - high.astype(F32)
-        mid = rest.astype(BF16)
-        low = (rest - mid.astype(F32)).astype(BF16)
-        lines.append(
-            jnp.concatenate([jnp.concatenate([high, mid, low], axis=1), spare], axis=0)
-        )
-    lanes_sum = lax.dot_general(
-        jnp.ones((8, 384), BF16),
-        jnp.concatenate(lines, axis=0),
-        (((1,), (1,)), ((), ())),
-        preferred_element_type=F32,
-    )
-    row4 = iota((4, 128), 0)
+        flat = jnp.where(lane80 == v, jnp.sum(s, axis=1, keepdims=True), flat)
+    flat = jnp.concatenate([flat, jnp.zeros((128 - total_members, 128), F32)], axis=0)
+    base = jnp.transpose(flat)[0:4]
     lane4 = iota((4, 128), 1)
-    base = jnp.zeros((4, 128), F32)
-    for v in range(variables):
-        base = jnp.where(row4 == v, lanes_sum[0:4, v * 128 : (v + 1) * 128], base)
     sums_src[0] = base
     here_z = zi * nc + ci
     mz[pl.ds(here_z, 1)] = base[None]
@@ -246,8 +232,10 @@
             return pl.ds(c * double + first, size)
 
         far = nz - 2
-        send(obs.at[double_at(2, n_up, n_down)], far_down, ob_sem.at[0], ob_sem.at[1], z_peer(2))
-        send(obs.at[double_at(far, 0, n_up)], far_up, ob_sem.at[2], ob_sem.at[3], z_peer(far))
+        if n_down:
+            send(obs.at[double_at(2, n_up, n_down)], far_down, ob_sem.at[0], ob_sem.at[1], z_peer(2))
+        if n_up:
+            send(obs.at[double_at(far, 0, n_up)], far_up, ob_sem.at[2], ob_sem.at[3], z_peer(far))
         if n_single:
             for d in ring_order(nz):
                 there = pl.ds(single_base + lax.rem(zi + d, nz) * n_single, n_single)
@@ -257,7 +245,8 @@
             send(source, near.at[slot], ob_sem.at[4], ob_sem.at[5], z_peer(d))
 
     landed(obs, load_sem.at[6 + variables])
-    if EARLY:
+    @pl.when(ci != lead)
+    def _():
         obs_copies()
 
     landed(innov, load_sem.at[2])
@@ -362,7 +351,8 @@
         for d in ring_order(ny):
             y_copy(d).start()
 
-    if not EARLY:
+    @pl.when(ci == lead)
+    def _():
         obs_copies()
 
     @pl.when(ci == lead)
@@ -378,8 +368,10 @@
                 if d or core != lead:
                     x_copy(d, core).start()
 
-    landed(far_down, ob_sem.at[1])
-    landed(far_up, ob_sem.at[3])
+    if n_down:
+        landed(far_down, ob_sem.at[1])
+    if n_up:
+        landed(far_up, ob_sem.at[3])
     landed(near.at[pl.ds(0, 2)], ob_sem.at[5])
     if n_single:
         landed(single.at[pl.ds(0, nz - 1)], ob_sem.at[7])
@@ -414,25 +406,32 @@
     keep = lax.rem(iota(tall.shape, 0), eight) == lax.rem(iota(tall.shape, 1), eight)
     wd = jnp.where(keep, tall, 0.0).astype(BF16)
 
-    for p in range(pieces):
-        if p < double:
-            first = 0 if p < n_up else pitch
-            answered = jnp.dot(
-                wd[:, first : first + width], packed[p], preferred_element_type=F32
-            )
-        else:
-            answered = jnp.dot(
-                wd[:, 2 * pitch :], packed_single[p - double], preferred_element_type=F32
-            )
-        resp_src[:, p] = answered.astype(BF16).reshape(nz, pair * eight, rows)
-        for d in ring_order(nz):
-            send(
-                resp_src.at[lax.rem(zi + d, nz), p],
-                resp_in.at[zi, p],
-                rs_sem.at[pieces],
-                rs_sem.at[p],
-                z_peer(d),
-            )
+    def respond(pieces_here):
+        for p in pieces_here:
+            if p < double:
+                first = 0 if p < n_up else pitch
+                answered = jnp.dot(
+                    wd[:, first : first + width], packed[p], preferred_element_type=F32
+                )
+            else:
+                answered = jnp.dot(
+                    wd[:, 2 * pitch :], packed_single[p - double], preferred_element_type=F32
+                )
+            resp_src[:, p] = answered.astype(BF16).reshape(nz, pair * eight, rows)
+            if p != double - 1 and p != pieces - 1:
+                continue
+            first = 0 if p < double else double
+            ready = pl.ds(first, p + 1 - first)
+            for d in ring_order(nz):
+                send(
+                    resp_src.at[lax.rem(zi + d, nz), ready],
+                    resp_in.at[zi, ready],
+                    rs_sem.at[2],
+                    rs_sem.at[first // double],
+                    z_peer(d),
+                )
+
+    respond(range(double))
 
     g_all = mx[0]
     for x in range(1, nx):
@@ -458,6 +457,8 @@
         other = lax.rem(zi + d, nz)
         send(pt_src.at[other, top], pt_in.at[zi, top], pt_sem.at[0], pt_sem.at[1], z_peer(d))
     pt_in[pl.ds(zi, 1), 0:pair, :] = pt_src[pl.ds(zi, 1), 0:pair, :]
+
+    respond(range(double, pieces))
     resp_in[pl.ds(zi, 1)] = resp_src[pl.ds(zi, 1)]
 
     def place(value, group):
@@ -471,7 +472,10 @@
                 ]
 
     for p in range(pieces):
-        landed(resp_in.at[pl.ds(0, nz - 1), p], rs_sem.at[p])
+        if p == 0:
+            landed(resp_in.at[pl.ds(0, nz - 1), pl.ds(0, double)], rs_sem.at[0])
+        elif p == double:
+            landed(resp_in.at[pl.ds(0, nz - 1), pl.ds(double, n_single)], rs_sem.at[1])
         if p < double:
             for c in range(owners):
                 value = resp_in[c, p].astype(F32) + resp_in[c + owners, p].astype(F32)
@@ -485,12 +489,14 @@
         whole = whole + pt_in[z, 0:pair, :]
     tot_ref[...] = whole[:, 0:NTYPES] / total_scale
 
-    landed(far_down, ob_sem.at[0])
-    landed(far_up, ob_sem.at[2])
+    if n_down:
+        landed(far_down, ob_sem.at[0])
+    if n_up:
+        landed(far_up, ob_sem.at[2])
     landed(near.at[pl.ds(0, 2)], ob_sem.at[4])
     if n_single:
         landed(single.at[pl.ds(0, nz - 1)], ob_sem.at[6])
-    landed(resp_src.at[pl.ds(0, nz - 1)], rs_sem.at[pieces])
+    landed(resp_src.at[pl.ds(0, nz - 1)], rs_sem.at[2])
     landed(pt_src.at[pl.ds(0, nz - 1), top], pt_sem.at[0])
 
     @pl.when(ci != lead)
@@ -604,8 +610,8 @@
             table((4, 4, 128), F32),
             table((1, 4, 128), F32),
             table((3, double, local_members, 8, rows), BF16),
-            table((n_up, local_members, 8, rows), BF16),
-            table((n_down, local_members, 8, rows), BF16),
+            table((max(n_up, 1), local_members, 8, rows), BF16),
+            table((max(n_down, 1), local_members, 8, rows), BF16),
             table((nz, max(n_single, 1), local_members, 8, rows), BF16),
             table((double, 32 * local_members, rows), BF16),
             table((max(n_single, 1), 8 * nz * local_members, rows), BF16),
@@ -619,7 +625,7 @@
             dma((2,)),
             dma((2,)),
             dma((8,)),
-            dma((pieces + 1,)),
+            dma((3,)),
             dma((2,)),
         ],
         compiler_params=pltpu.CompilerParams(

time: 36.6 us -> 35.9 us (0.981)
  Pallas kernels: 35.8 us -> 35.1 us
    pallas_call x1, Pallas kernels: 35.1 us -> 34.3 us  [local(): pl.pallas_call(functools.partial(exchange_kernel, dims, (variables, membe...]
where the time goes in v5:
time: 35.9 us; the launch traced here: 35.7 us
  Pallas kernels  35.1 us (98%)
  between operations  0.64 us (2%)
    pallas_call x1, Pallas kernels, local(): pl.pallas_call(functools.partial(exchange_kernel, dims, (variables, membe...  34.3 us
    pallas_call x1, Pallas kernels, local(): pl.pallas_call(store_kernel, out_shape=(pltpu.HBM(out.shape, F32), pltpu....  0.72 us

profile of v5, /device:TPU:1, one launch (start us, length us, event | category | flops | bytes accessed | tf_op | source)
XLA Modules:
  0.0 35.7 jit_solution(16353638720656281835)
XLA Ops:
  0.6 34.3 %shard_map.104 = (f32[512,128]{1,0:T(8,128)S(1)}, f32[2,8]{1,0:T(2,128)S(1)}) custom-call(bf16[4,40,48,128]{3,2,1,0:T(8,128)(2,1)} %bitcast.27, f32[4,24,128]{2,1,0:T(8,128)} %bitcast.29, f32[4,24,128]{2,1,0:T(8,128)} %bitcast.30, f32[1,4]{1,0:T(1,128)} %bitcast.31, bf16[10,16,8,256]{3,2,1,0:T(8,128)(2,1)} %bitcast.28, f32[128,256]{1,0:T(8,128)} %innov_ref.1, ...), custom_call_target="tpu_custom_call" | custom-call | tf_op jit(solution)/shard_map/pallas_call | solution.py:578
  35.0 0.7 %shard_map.105 = (f32[512,128]{1,0:T(8,128)}, f32[2,8]{1,0:T(2,128)}) custom-call(f32[512,128]{1,0:T(8,128)S(1)} %get-tuple-element.6.out_ref, f32[2,8]{1,0:T(2,128)S(1)} %get-tuple-element.7.tot_ref), custom_call_target="tpu_custom_call" | custom-call | tf_op jit(solution)/shard_map/pallas_call | solution.py:635

commit v6 on v5

--- a/solution.py
+++ b/solution.py
@@ -161,10 +161,10 @@
     load(now_ref, errors.at[0], 0)
     load(prior_ref, errors.at[1], 0)
     load(energy_ref, energy, 1)
-    for v in range(variables):
-        load(anom_ref.at[v], anom.at[v], 6 + v)
+    for v in range(0, variables, 2):
+        load(anom_ref.at[pl.ds(v, 2)], anom.at[pl.ds(v, 2)], 6 + v // 2)
     for m in range(members):
-        load(obs_ref.at[m], obs.at[:, m], 6 + variables)
+        load(obs_ref.at[m], obs.at[:, m], 6 + variables // 2)
     load(innov_ref, innov, 2)
     load(valid_ref, valid, 3)
     load(type_ref, types, 4)
@@ -181,7 +181,8 @@
     for v in range(variables):
         grad = energy[0:1, v : v + 1] * cosine * (errors[0, v] + errors[1, v])
         grad = grad.astype(BF16).astype(F32)
-        landed(anom.at[v], load_sem.at[6 + v])
+        if v % 2 == 0:
+            landed(anom.at[pl.ds(v, 2)], load_sem.at[6 + v // 2])
         step = 4
         for k in range(0, anom.shape[1], step):
             a = anom[v, k : k + step].astype(F32)
@@ -244,7 +245,7 @@
             source = obs.at[double_at(d, 0, double)]
             send(source, near.at[slot], ob_sem.at[4], ob_sem.at[5], z_peer(d))
 
-    landed(obs, load_sem.at[6 + variables])
+    landed(obs, load_sem.at[6 + variables // 2])
     @pl.when(ci != lead)
     def _():
         obs_copies()
@@ -305,7 +306,8 @@
         )
         return ((iota((128, pitch), 0) == wanted) & (spot < width)).astype(BF16)
 
-    tables = [select(-1), select(-2)]
+    tables = ([select(-1)] if n_up else []) + ([select(-2)] if n_down else [])
+    doubles = len(tables)
     if n_single:
         shape = (128, nz * one)
         tables.append((iota(shape, 0) == iota(shape, 1) // eight).astype(BF16))
@@ -409,13 +411,13 @@
     def respond(pieces_here):
         for p in pieces_here:
             if p < double:
-                first = 0 if p < n_up else pitch
+                first = 0 if p < n_up or doubles == 1 else pitch
                 answered = jnp.dot(
                     wd[:, first : first + width], packed[p], preferred_element_type=F32
                 )
             else:
                 answered = jnp.dot(
-                    wd[:, 2 * pitch :], packed_single[p - double], preferred_element_type=F32
+                    wd[:, doubles * pitch :], packed_single[p - double], preferred_element_type=F32
                 )
             resp_src[:, p] = answered.astype(BF16).reshape(nz, pair * eight, rows)
             if p != double - 1 and p != pieces - 1:
@@ -619,7 +621,7 @@
             table((nz, pieces, pair * 8, rows), BF16),
             table((nz, 8, 128), F32),
             table((nz, 8, 128), F32),
-            dma((7 + variables,)),
+            dma((7 + variables // 2,)),
             dma((2,)),
             dma((2,)),
             dma((2,)),

time: 35.9 us -> 35.8 us (level)
  no operation moved by 1% of the time
where the time goes in v6:
time: 35.8 us; the launch traced here: 35.7 us
  Pallas kernels  35 us (98%)
  between operations  0.64 us (2%)
    pallas_call x1, Pallas kernels, local(): pl.pallas_call(functools.partial(exchange_kernel, dims, (variables, membe...  34.3 us
    pallas_call x1, Pallas kernels, local(): pl.pallas_call(store_kernel, out_shape=(pltpu.HBM(out.shape, F32), pltpu....  0.72 us

profile of v6, /device:TPU:1, one launch (start us, length us, event | category | flops | bytes accessed | tf_op | source)
XLA Modules:
  0.0 35.7 jit_solution(9685035499800518458)
XLA Ops:
  0.6 34.3 %shard_map.104 = (f32[512,128]{1,0:T(8,128)S(1)}, f32[2,8]{1,0:T(2,128)S(1)}) custom-call(bf16[4,40,48,128]{3,2,1,0:T(8,128)(2,1)} %bitcast.27, f32[4,24,128]{2,1,0:T(8,128)} %bitcast.29, f32[4,24,128]{2,1,0:T(8,128)} %bitcast.30, f32[1,4]{1,0:T(1,128)} %bitcast.31, bf16[10,16,8,256]{3,2,1,0:T(8,128)(2,1)} %bitcast.28, f32[128,256]{1,0:T(8,128)} %innov_ref.1, ...), custom_call_target="tpu_custom_call" | custom-call | tf_op jit(solution)/shard_map/pallas_call | solution.py:580
  34.9 0.7 %shard_map.105 = (f32[512,128]{1,0:T(8,128)}, f32[2,8]{1,0:T(2,128)}) custom-call(f32[512,128]{1,0:T(8,128)S(1)} %get-tuple-element.6.out_ref, f32[2,8]{1,0:T(2,128)S(1)} %get-tuple-element.7.tot_ref), custom_call_target="tpu_custom_call" | custom-call | tf_op jit(solution)/shard_map/pallas_call | solution.py:637
